TPU v7x, 64 devices: a 2x2x8 block of a 4x4x8 slice. The times are simulated.
64 devices in a mesh: rep: 4 (over x, y), dp: 16 (over z, core).
Axes of the slice: x: 2, y: 2, z: 8, core: 2. Of those that a mesh axis runs over, the one named last changes fastest.
The devices are a block of a 4x4x8 slice.
Arguments:
- x: bfloat16 [64, 2048, 640], P(('rep', 'dp')), parts along dimension 0
- dy: bfloat16 [64, 2048, 640], P(('rep', 'dp')), parts along dimension 0
- w_gate: bfloat16 [2, 640, 2048], P(None, 'dp')
- w_up: bfloat16 [2, 640, 2048], P(None, 'dp')
- w_down: bfloat16 [2, 2048, 640], P(None, 'dp')
- m_w_gate: float32 [2, 640, 2048], P(None, 'dp')
- m_w_up: float32 [2, 640, 2048], P(None, 'dp')
- m_w_down: float32 [2, 2048, 640], P(None, 'dp')
- v_w_gate: float32 [2, 640, 2048], P(None, 'dp')
- v_w_up: float32 [2, 640, 2048], P(None, 'dp')
- v_w_down: float32 [2, 2048, 640], P(None, 'dp')
Outputs:
- output 1: bfloat16 [8, 640, 2048], P('rep', 'dp'), parts along dimension 0
- output 2: bfloat16 [8, 640, 2048], P('rep', 'dp'), parts along dimension 0
- output 3: bfloat16 [8, 2048, 640], P('rep', 'dp'), parts along dimension 0
- output 4: float32 [8, 640, 2048], P('rep', 'dp'), parts along dimension 0
- output 5: float32 [8, 640, 2048], P('rep', 'dp'), parts along dimension 0
- output 6: float32 [8, 2048, 640], P('rep', 'dp'), parts along dimension 0
- output 7: float32 [8, 640, 2048], P('rep', 'dp'), parts along dimension 0
- output 8: float32 [8, 640, 2048], P('rep', 'dp'), parts along dimension 0
- output 9: float32 [8, 2048, 640], P('rep', 'dp'), parts along dimension 0
There are 4 independent parts. A program takes and returns all parts, laid end to end along the dimension named above; an argument that names none is the same for every part.
All inputs are finite; a program needn't handle non-finite values.
Results may differ from a plain program's by a relative error of at most 0.0228.
Values are sent between devices in bfloat16 or wider.
A program may use at most 768 MiB of HBM per device.

v0:
```python
import jax
import jax.numpy as jnp
from jax import lax
from jax.sharding import PartitionSpec as P

NAMES = ("w_gate", "w_up", "w_down")


def matmul(a, w):
    return jnp.dot(a, w, preferred_element_type=jnp.float32).astype(jnp.bfloat16)


def normed(h):
    wide = h.astype(jnp.float32)
    scale = lax.rsqrt(jnp.mean(wide**2, -1, keepdims=True) + 1e-6)
    return (wide * scale).astype(jnp.bfloat16)


def layer(h, w):
    a = normed(h)
    gate = jnp.dot(a, w["w_gate"], preferred_element_type=jnp.float32)
    up = jnp.dot(a, w["w_up"], preferred_element_type=jnp.float32)
    return h + matmul((jax.nn.silu(gate) * up).astype(jnp.bfloat16), w["w_down"])


def adamw(w, m, v, g):
    m = 0.9 * m + 0.1 * g
    v = 0.95 * v + 0.05 * g * g
    step = m * lax.rsqrt(v + 1e-8) + 0.1 * w
    return (w - 0.02 * step).astype(jnp.bfloat16), m, v


def clipped(gradients, sum_of_squares, count):
    factor = jnp.minimum(1.0, 0.5 * lax.rsqrt(sum_of_squares / count + 1e-30))
    return [g * factor for g in gradients]


def solution(mesh):
    def fetched(weights, number):
        return {name: lax.all_gather(w[number], "dp", axis=0, tiled=True) for name, w in zip(NAMES, weights, strict=True)}

    def step(x, dy, *arrays):
        weights, m, v = (arrays[i : i + 3] for i in (0, 3, 6))
        layers = weights[0].shape[0]
        h, kept = x[0], []
        for number in range(layers):
            kept.append(h)
            h = layer(h, fetched(weights, number))
        by_h, mine = dy[0], [None] * layers
        for number in reversed(range(layers)):
            _, back = jax.vjp(lambda w, h: layer(h, w), fetched(weights, number), kept[number])
            by_w, by_h = back(by_h)
            mine[number] = [lax.psum_scatter(by_w[name], "dp", scatter_dimension=0, tiled=True) for name in NAMES]
        gradients = [jnp.stack([mine[number][i] for number in range(layers)]).astype(jnp.float32) for i in range(3)]
        squares = lax.psum(sum(jnp.sum(g * g) for g in gradients), "dp")
        gradients = clipped(gradients, squares, lax.psum(1, "dp") * sum(g.size for g in gradients))
        new = [adamw(w.astype(jnp.float32), m, v, g) for w, m, v, g in zip(weights, m, v, gradients, strict=True)]
        return tuple(one[which] for which in range(3) for one in new)

    states, cut = P(("rep", "dp"), None, None), P(None, "dp", None)
    return jax.shard_map(
        step,
        mesh=mesh,
        in_specs=(states, states) + (cut,) * 9,
        out_specs=(P("rep", "dp", None),) * 9,
        check_vma=False,
    )
```

profile of v0, /device:TPU:21, one launch (start us, length us, event | category | flops | bytes accessed | tf_op | source)
XLA Modules:
  0.0 683.7 jit_solution(432608990110943485)
XLA Ops:
  7.3 1.7 fusion.94
  9.1 0.1 all-gather.15.cloned.1.call-start
  9.1 1.7 fusion.93
  10.9 0.1 all-gather.17.cloned.1.call-start
  11.0 1.7 fusion.92
  12.9 0.6 all-gather.21.cloned.1.call-update
  13.5 0.6 all-gather.23.cloned.1.call-update
  14.2 0.6 all-gather.19.cloned.1.call-update
  14.8 3.0 copy.20
  17.8 0.6 fusion.15
  18.4 4.8 copy.21
  23.2 28.7 %all-gather.13.cloned.1.call-done = bf16[1,640,2048]{2,1,0:T(8,128)(2,1)} async-done(((bf16[1,40,2048]{2,1,0:T(8,128)(2,1)}), bf16[1,640,2048]{2,1,0:T(8,128)(2,1)}) %all-gather.13.cloned.1.call-update) | async-done | bytes 2621456 | tf_op jit(solution)/shard_map/all_gather | solution.py:40
  51.9 11.9 %fusion.44 = f32[2048,2048]{1,0:T(8,128)} fusion(bf16[1,640,2048]{2,1,0:T(8,128)(2,1)} %all-gather.13.cloned.1.call-done, bf16[1,2048,640]{1,2,0:T(8,128)(2,1)S(1)} %copy.20, f32[2048]{0:T(1024)S(1)} %add_rsqrt_fusion), kind=kOutput, calls=%fused_computation.63 | convolution fusion | flops 5372641280 | bytes 22028288 | tf_op jit(solution)/shard_map/dot_general | solution.py:21
  63.8 25.4 %all-gather.15.cloned.1.call-done = bf16[1,640,2048]{2,1,0:T(8,128)(2,1)} async-done(((bf16[1,40,2048]{2,1,0:T(8,128)(2,1)}), bf16[1,640,2048]{2,1,0:T(8,128)(2,1)}) %all-gather.15.cloned.1.call-update) | async-done | bytes 2621456 | tf_op jit(solution)/shard_map/all_gather | solution.py:40
  89.2 17.8 %multiply_convert_fusion.1 = (bf16[2048,2048]{1,0:T(8,128)(2,1)}, f32[2048,2048]{1,0:T(8,128)}) fusion(f32[2048,2048]{1,0:T(8,128)} %fusion.44, bf16[1,640,2048]{2,1,0:T(8,128)(2,1)} %all-gather.15.cloned.1.call-done, bf16[1,2048,640]{1,2,0:T(8,128)(2,1)S(1)} %copy.20, f32[2048]{0:T(1024)S(1)} %add_rsqrt_fusion), kind=kOutput, calls=%fused_computation.17 | convolution fusion | flops 5397807104 | bytes 47194112 | tf_op jit(solution)/shard_map/dot_general | solution.py:22
  107.0 19.6 %all-gather.17.cloned.1.call-done = bf16[1,2048,640]{2,1,0:T(8,128)(2,1)} async-done(((bf16[1,128,640]{2,1,0:T(8,128)(2,1)}), bf16[1,2048,640]{2,1,0:T(8,128)(2,1)}) %all-gather.17.cloned.1.call-update) | async-done | bytes 2621456 | tf_op jit(solution)/shard_map/all_gather | solution.py:40
  126.5 10.4 %fusion.19 = (f32[2048]{0:T(1024)S(1)}, bf16[2048,640]{0,1:T(8,128)(2,1)}) fusion(bf16[2048,2048]{1,0:T(8,128)(2,1)} %get-tuple-element.24, bf16[1,2048,640]{2,1,0:T(8,128)(2,1)} %all-gather.17.cloned.1.call-done, bf16[1,2048,640]{1,2,0:T(8,128)(2,1)S(1)} %copy.20), kind=kOutput, calls=%fused_computation.37 | convolution fusion | flops 5375260672 | bytes 16261120 | tf_op jit(solution)/shard_map/dot_general | solution.py:10
  137.0 26.7 %all-gather.21.cloned.1.call-done = bf16[1,2048,640]{2,1,0:T(8,128)(2,1)} async-done(((bf16[1,128,640]{2,1,0:T(8,128)(2,1)}), bf16[1,2048,640]{2,1,0:T(8,128)(2,1)}) %all-gather.21.cloned.1.call-update) | async-done | bytes 2621456 | tf_op jit(solution)/shard_map/all_gather | solution.py:40
  163.7 11.2 %convolution_convert_fusion.1 = bf16[2048,2048]{1,0:T(8,128)(2,1)} fusion(bf16[1,2048,640]{2,1,0:T(8,128)(2,1)} %param.12, bf16[1,2048,640]{2,1,0:T(8,128)(2,1)} %all-gather.21.cloned.1.call-done), kind=kOutput, calls=%fused_computation.29 | convolution fusion | flops 5372903424 | bytes 13631488 | tf_op jit(solution)/shard_map/transpose(jvp())/dot_general | solution.py:10
  174.9 26.0 %all-gather.23.cloned.1.call-done = bf16[1,640,2048]{2,1,0:T(8,128)(2,1)} async-done(((bf16[1,40,2048]{2,1,0:T(8,128)(2,1)}), bf16[1,640,2048]{2,1,0:T(8,128)(2,1)}) %all-gather.23.cloned.1.call-update) | async-done | bytes 2621456 | tf_op jit(solution)/shard_map/all_gather | solution.py:40
  200.9 11.9 %fusion.33 = f32[2048,2048]{1,0:T(8,128)} fusion(bf16[1,640,2048]{2,1,0:T(8,128)(2,1)} %all-gather.23.cloned.1.call-done, bf16[2048,640]{0,1:T(8,128)(2,1)S(1)} %copy-done.3, f32[2048]{0:T(1024)S(1)} %fusion.80), kind=kOutput, calls=%fused_computation.52 | convolution fusion | flops 5372641280 | bytes 22028288 | tf_op jit(solution)/shard_map/jvp()/dot_general | solution.py:22
  212.8 25.2 %all-gather.19.cloned.1.call-done = bf16[1,640,2048]{2,1,0:T(8,128)(2,1)} async-done(((bf16[1,40,2048]{2,1,0:T(8,128)(2,1)}), bf16[1,640,2048]{2,1,0:T(8,128)(2,1)}) %all-gather.19.cloned.1.call-update) | async-done | bytes 2621456 | tf_op jit(solution)/shard_map/all_gather | solution.py:40
  238.1 23.4 %fusion.2 = (bf16[2048,2048]{1,0:T(8,128)(2,1)}, f32[2048,2048]{1,0:T(8,128)}) fusion(f32[2048,2048]{1,0:T(8,128)} %fusion.33, bf16[2048,2048]{1,0:T(8,128)(2,1)} %convolution_convert_fusion.1, bf16[1,640,2048]{2,1,0:T(8,128)(2,1)} %all-gather.19.cloned.1.call-done, bf16[2048,640]{0,1:T(8,128)(2,1)S(1)} %copy-done.3, f32[2048]{0:T(1024)S(1)} %fusion.80), kind=kOutput, calls=%fused_computation.8 | convolution fusion | flops 5422972928 | bytes 55582720 | tf_op jit(solution)/shard_map/jvp()/dot_general | solution.py:21
  261.5 12.2 %fusion.23 = bf16[2048,640]{0,1:T(8,128)(2,1)S(1)} fusion(bf16[2048,2048]{1,0:T(8,128)(2,1)} %convolution_convert_fusion.1, bf16[1,640,2048]{2,1,0:T(8,128)(2,1)} %all-gather.23.cloned.1.call-done, f32[2048,2048]{1,0:T(8,128)} %get-tuple-element.29), kind=kOutput, calls=%fused_computation.41 | convolution fusion | flops 5395185664 | bytes 30408704 | tf_op jit(solution)/shard_map/transpose(jvp())/dot_general | solution.py:22
  273.7 6.2 fusion.21
  279.9 1.8 fusion.30
  281.7 1.5 copy-done.4
  283.3 10.6 %convolution_convert_fusion.2 = bf16[2048,640]{1,0:T(8,128)(2,1)} fusion(bf16[2048,2048]{1,0:T(8,128)(2,1)} %get-tuple-element.24, bf16[2048,640]{0,1:T(8,128)(2,1)S(1)} %fusion.30), kind=kOutput, calls=%fused_computation.45 | convolution fusion | flops 5370019840 | bytes 13631488 | tf_op jit(solution)/shard_map/transpose(jvp())/dot_general | solution.py:10
  293.9 0.1 reduce-scatter.17.cloned.1.call-start
  294.0 15.6 %fusion.22 = bf16[2048,640]{1,0:T(8,128)(2,1)} fusion(f32[2048,2048]{1,0:T(8,128)} %fusion.33, bf16[1,2048,640]{2,1,0:T(8,128)(2,1)S(1)} %copy-done.5, f32[2048,2048]{1,0:T(8,128)} %get-tuple-element.29), kind=kOutput, calls=%fused_computation.40 | convolution fusion | flops 5395185664 | bytes 38797312 | tf_op jit(solution)/shard_map/transpose(jvp())/dot_general | solution.py:10
  309.7 9.5 %convolution_convert_fusion = bf16[2048,2048]{1,0:T(8,128)(2,1)S(1)} fusion(bf16[2048,640]{0,1:T(8,128)(2,1)} %copy-done.4, bf16[1,2048,640]{2,1,0:T(8,128)(2,1)} %all-gather.17.cloned.1.call-done), kind=kOutput, calls=%fused_computation.28 | convolution fusion | flops 5372903424 | bytes 13631488 | tf_op jit(solution)/shard_map/transpose(jvp())/dot_general | solution.py:10
  319.3 3.2 copy-done.15
  322.5 11.0 %fusion.28 = bf16[640,2048]{1,0:T(8,128)(2,1)} fusion(bf16[2048,2048]{1,0:T(8,128)(2,1)S(1)} %convolution_convert_fusion, f32[2048,2048]{1,0:T(8,128)} %fusion.44, bf16[1,2048,640]{1,2,0:T(8,128)(2,1)S(1)} %copy-done.2, f32[2048]{0:T(1024)S(1)} %copy-done.13), kind=kOutput, calls=%fused_computation.44 | convolution fusion | flops 5399117824 | bytes 30416896 | tf_op jit(solution)/shard_map/transpose(jvp())/dot_general | solution.py:22
  333.6 13.3 %fusion.24 = bf16[640,2048]{1,0:T(8,128)(2,1)} fusion(bf16[2048,2048]{1,0:T(8,128)(2,1)} %convolution_convert_fusion.1, bf16[2048,640]{0,1:T(8,128)(2,1)} %get-tuple-element.27, f32[2048]{0:T(1024)S(1)} %fusion.80, f32[2048,2048]{1,0:T(8,128)} %get-tuple-element.29), kind=kOutput, calls=%fused_computation.42 | convolution fusion | flops 5399117824 | bytes 30416896 | tf_op jit(solution)/shard_map/transpose(jvp())/dot_general | solution.py:22
  347.0 19.4 %fusion.25 = bf16[640,2048]{1,0:T(8,128)(2,1)} fusion(f32[2048,2048]{1,0:T(8,128)} %fusion.44, f32[2048,2048]{1,0:T(8,128)} %get-tuple-element.25, bf16[2048,2048]{1,0:T(8,128)(2,1)} %copy-done.15, bf16[1,2048,640]{1,2,0:T(8,128)(2,1)S(1)} %copy-done.2, f32[2048]{0:T(1024)S(1)} %copy-done.13), kind=kOutput, calls=%fused_computation.43 | convolution fusion | flops 5420089344 | bytes 47194112 | tf_op jit(solution)/shard_map/transpose(jvp())/dot_general | solution.py:21
  366.5 0.1 reduce-scatter.9.cloned.1.call-start
  366.5 10.6 %convolution_convert_fusion.3 = bf16[640,2048]{1,0:T(8,128)(2,1)} fusion(bf16[2048,2048]{1,0:T(8,128)(2,1)} %get-tuple-element.28, bf16[2048,640]{0,1:T(8,128)(2,1)} %get-tuple-element.27, f32[2048]{0:T(1024)S(1)} %fusion.80), kind=kOutput, calls=%fused_computation.46 | convolution fusion | flops 5372641280 | bytes 13639680 | tf_op jit(solution)/shard_map/transpose(jvp())/dot_general | solution.py:21
  377.3 28.0 %reduce-scatter.17.cloned.1.call-done = bf16[128,640]{1,0:T(8,128)(2,1)} async-done(((bf16[2048,640]{1,0:T(8,128)(2,1)}), bf16[128,640]{1,0:T(8,128)(2,1)}) %reduce-scatter.17.cloned.1.call-update) | async-done | bytes 163856 | tf_op jit(solution)/shard_map/reduce_scatter | solution.py:53
  405.3 1.8 fusion.70
  407.1 56.5 %reduce-scatter.11.cloned.1.call-done = bf16[40,2048]{1,0:T(8,128)(2,1)} async-done(((bf16[640,2048]{1,0:T(8,128)(2,1)}), bf16[40,2048]{1,0:T(8,128)(2,1)}) %reduce-scatter.11.cloned.1.call-update) | async-done | bytes 163856 | tf_op jit(solution)/shard_map/reduce_scatter | solution.py:53
  463.6 58.3 %reduce-scatter.13.cloned.1.call-done = bf16[40,2048]{1,0:T(8,128)(2,1)} async-done(((bf16[640,2048]{1,0:T(8,128)(2,1)}), bf16[40,2048]{1,0:T(8,128)(2,1)}) %reduce-scatter.13.cloned.1.call-update) | async-done | bytes 163856 | tf_op jit(solution)/shard_map/reduce_scatter | solution.py:53
  521.9 1.8 fusion.69
  523.6 56.7 %reduce-scatter.7.cloned.1.call-done = bf16[40,2048]{1,0:T(8,128)(2,1)} async-done(((bf16[640,2048]{1,0:T(8,128)(2,1)}), bf16[40,2048]{1,0:T(8,128)(2,1)}) %reduce-scatter.7.cloned.1.call-update) | async-done | bytes 163856 | tf_op jit(solution)/shard_map/reduce_scatter | solution.py:53
  580.3 58.3 %reduce-scatter.9.cloned.1.call-done = bf16[40,2048]{1,0:T(8,128)(2,1)} async-done(((bf16[640,2048]{1,0:T(8,128)(2,1)}), bf16[40,2048]{1,0:T(8,128)(2,1)}) %reduce-scatter.9.cloned.1.call-update) | async-done | bytes 163856 | tf_op jit(solution)/shard_map/reduce_scatter | solution.py:53
  638.6 1.8 fusion.68
  642.3 27.1 %psum.7 = f32[]{:T(128)} all-reduce(f32[]{:T(128)S(6)} %add.99), channel_id=1, replica_groups=mesh['rep'=4,'dp'=16] {'dp'}, use_global_device_ids=true, to_apply=%region_12.13 | all-reduce | flops 1 | bytes 8 | tf_op jit(solution)/shard_map/psum | solution.py:55
  670.1 2.8 fusion.76
  672.9 3.5 fusion.67
  (53 shorter events, 1.1 us)
Async XLA Ops:
  7.2 44.7 %all-gather.13.cloned.1.call-start = ((), (), s32[]{:S(2)}) async-start(), calls=%async_computation.12 | async-start | bytes 2785280 | tf_op jit(solution)/shard_map/all_gather | solution.py:40
  9.1 80.1 %all-gather.15.cloned.1.call-start = ((), (), s32[]{:S(2)}) async-start(), calls=%async_computation.13 | async-start | bytes 2785280 | tf_op jit(solution)/shard_map/all_gather | solution.py:40
  10.9 115.6 %all-gather.17.cloned.1.call-start = ((), (), s32[]{:S(2)}) async-start(), calls=%async_computation.14 | async-start | bytes 2785280 | tf_op jit(solution)/shard_map/all_gather | solution.py:40
  12.8 150.9 %all-gather.21.cloned.1.call-start = ((), (), s32[]{:S(2)}) async-start(), calls=%async_computation.16 | async-start | bytes 2785280 | tf_op jit(solution)/shard_map/all_gather | solution.py:40
  13.5 187.4 %all-gather.23.cloned.1.call-start = ((), (), s32[]{:S(2)}) async-start(), calls=%async_computation.17 | async-start | bytes 2785280 | tf_op jit(solution)/shard_map/all_gather | solution.py:40
  14.1 224.0 %all-gather.19.cloned.1.call-start = ((), (), s32[]{:S(2)}) async-start(), calls=%async_computation.15 | async-start | bytes 2785280 | tf_op jit(solution)/shard_map/all_gather | solution.py:40
  14.7 362.6 %reduce-scatter.15.cloned.1.call-start = ((), (), s32[]{:S(2)}) async-start(), calls=%async_computation.10 | async-start | bytes 2785280 | tf_op jit(solution)/shard_map/reduce_scatter | solution.py:53
  17.8 108.7 %copy-start.1 = (bf16[1,2048,640]{1,2,0:T(8,128)(2,1)}, bf16[1,2048,640]{1,2,0:T(8,128)(2,1)S(1)}, u32[]{:S(2)}) copy-start(bf16[1,2048,640]{1,2,0:T(8,128)(2,1)S(1)} %copy.20) | copy-start | bytes 7864324
  18.4 70.8 %copy-start.12 = (f32[2048]{0:T(1024)}, f32[2048]{0:T(1024)S(1)}, u32[]{:S(2)}) copy-start(f32[2048]{0:T(1024)S(1)} %add_rsqrt_fusion) | copy-start | bytes 24580
  137.0 63.9 %copy-start.3 = (bf16[2048,640]{0,1:T(8,128)(2,1)S(1)}, bf16[2048,640]{0,1:T(8,128)(2,1)}, u32[]{:S(2)}) copy-start(bf16[2048,640]{0,1:T(8,128)(2,1)} %get-tuple-element.27) | copy-start | bytes 7864324
  261.5 12.2 %copy-start.14 = (bf16[1,640,2048]{2,1,0:T(8,128)(2,1)S(1)}, bf16[1,640,2048]{2,1,0:T(8,128)(2,1)}, u32[]{:S(2)}) copy-start(bf16[1,640,2048]{2,1,0:T(8,128)(2,1)} %all-gather.19.cloned.1.call-done) | copy-start | bytes 7864324
  261.5 12.2 %copy-start.16 = (bf16[2048,2048]{1,0:T(8,128)(2,1)S(1)}, bf16[2048,2048]{1,0:T(8,128)(2,1)}, u32[]{:S(2)}) copy-start(bf16[2048,2048]{1,0:T(8,128)(2,1)} %get-tuple-element.28) | copy-start | bytes 25165828
  273.7 6.2 copy-start
  281.7 1.5 copy-start.4
  283.3 10.8 %copy-start.5 = (bf16[1,2048,640]{2,1,0:T(8,128)(2,1)S(1)}, bf16[1,2048,640]{2,1,0:T(8,128)(2,1)}, u32[]{:S(2)}) copy-start(bf16[1,2048,640]{2,1,0:T(8,128)(2,1)} %param.12) | copy-start | bytes 7864324
  293.9 111.4 %reduce-scatter.17.cloned.1.call-start = ((), (), s32[]{:S(2)}) async-start(), calls=%async_computation.11 | async-start | bytes 2785280 | tf_op jit(solution)/shard_map/reduce_scatter | solution.py:53
  309.6 12.9 %copy-start.2 = (bf16[1,2048,640]{1,2,0:T(8,128)(2,1)S(1)}, bf16[1,2048,640]{1,2,0:T(8,128)(2,1)}, u32[]{:S(2)}) copy-start(bf16[1,2048,640]{1,2,0:T(8,128)(2,1)} %copy-done.1) | copy-start | bytes 7864324
  309.7 12.9 %copy-start.13 = (f32[2048]{0:T(1024)S(1)}, f32[2048]{0:T(1024)}, u32[]{:S(2)}) copy-start(f32[2048]{0:T(1024)} %copy-done.12) | copy-start | bytes 24580
  309.7 153.9 %reduce-scatter.11.cloned.1.call-start = ((), (), s32[]{:S(2)}) async-start(), calls=%async_computation.8 | async-start | bytes 2785280 | tf_op jit(solution)/shard_map/reduce_scatter | solution.py:53
  319.3 3.3 copy-start.15
  333.6 188.3 %reduce-scatter.13.cloned.1.call-start = ((), (), s32[]{:S(2)}) async-start(), calls=%async_computation.9 | async-start | bytes 2785280 | tf_op jit(solution)/shard_map/reduce_scatter | solution.py:53
  347.0 233.3 %reduce-scatter.7.cloned.1.call-start = ((), (), s32[]{:S(2)}) async-start(), calls=%async_computation.6 | async-start | bytes 2785280 | tf_op jit(solution)/shard_map/reduce_scatter | solution.py:53
  366.5 303.6 %copy-start.8 = (bf16[2,128,640]{2,1,0:T(8,128)(2,1)S(1)}, bf16[2,128,640]{2,1,0:T(8,128)(2,1)}, u32[]{:S(2)}) copy-start(bf16[2,128,640]{2,1,0:T(8,128)(2,1)} %param.15) | copy-start | bytes 983044
  366.5 272.1 %reduce-scatter.9.cloned.1.call-start = ((), (), s32[]{:S(2)}) async-start(), calls=%async_computation.7 | async-start | bytes 2785280 | tf_op jit(solution)/shard_map/reduce_scatter | solution.py:53
  377.2 295.7 %copy-start.6 = (bf16[2,40,2048]{2,1,0:T(8,128)(2,1)S(1)}, bf16[2,40,2048]{2,1,0:T(8,128)(2,1)}, u32[]{:S(2)}) copy-start(bf16[2,40,2048]{2,1,0:T(8,128)(2,1)} %param.13) | copy-start | bytes 983044
  377.2 295.7 %copy-start.7 = (bf16[2,40,2048]{2,1,0:T(8,128)(2,1)S(1)}, bf16[2,40,2048]{2,1,0:T(8,128)(2,1)}, u32[]{:S(2)}) copy-start(bf16[2,40,2048]{2,1,0:T(8,128)(2,1)} %param.14) | copy-start | bytes 983044
  377.2 295.7 %copy-start.9 = (f32[2,40,2048]{2,1,0:T(8,128)S(1)}, f32[2,40,2048]{2,1,0:T(8,128)}, u32[]{:S(2)}) copy-start(f32[2,40,2048]{2,1,0:T(8,128)} %param.19) | copy-start | bytes 1966084
  377.2 295.7 %copy-start.10 = (f32[2,40,2048]{2,1,0:T(8,128)S(1)}, f32[2,40,2048]{2,1,0:T(8,128)}, u32[]{:S(2)}) copy-start(f32[2,40,2048]{2,1,0:T(8,128)} %param.16) | copy-start | bytes 1966084
  377.2 295.7 %copy-start.11 = (f32[2,40,2048]{2,1,0:T(8,128)S(1)}, f32[2,40,2048]{2,1,0:T(8,128)}, u32[]{:S(2)}) copy-start(f32[2,40,2048]{2,1,0:T(8,128)} %param.20) | copy-start | bytes 1966084
Sparse Core Ops, SparseCore 0:
  10.2 41.5 all-gather.12
  54.1 35.0 all-gather.14
  91.4 35.0 all-gather.16
  128.6 35.0 all-gather.20
  165.8 35.0 all-gather.22
  202.9 35.0 all-gather.18
  294.1 52.8 reduce-scatter.14
  349.3 56.0 reduce-scatter.16
  407.7 55.8 reduce-scatter.10
  465.8 56.0 reduce-scatter.12
  524.2 56.0 reduce-scatter.6
  582.5 56.0 reduce-scatter.8
where the time goes:
time: 692 us; the launch traced here: 684 us
  waiting for transfers between devices  412 us (60%)
  matrix products  195 us (28%)
  blocking collectives  27.1 us (4%)
  local copies, waits for them, and re-layouts  17.9 us (3%)
  between operations  17.5 us (3%)
  other arithmetic  14 us (2%)
    reduce_scatter x6, waiting for transfers between devices, step(): lax.psum_scatter(by_w[name], 'dp', scatter_dimension=0, tiled=True)  258 us
    all_gather x6, waiting for transfers between devices, fetched(): lax.all_gather(w[number], 'dp', axis=0, tiled=True)  152 us
    dot_general x5, matrix products, layer(): gate = jnp.dot(a, w['w_gate'], preferred_element_type=jnp.float32)  71.5 us
    dot_general x5, matrix products, layer(): up = jnp.dot(a, w['w_up'], preferred_element_type=jnp.float32)  66.1 us
    dot_general x5, matrix products, matmul(): jnp.dot(a, w, preferred_element_type=jnp.float32).astype(jnp.bfloat16)  57.3 us
    psum x1, blocking collectives, step(): squares = lax.psum(sum((jnp.sum(g * g) for g in gradients)), 'dp')  27.1 us
  transfers between devices with their start and end apart: 12, of which 11 were waited for; matrix products, arithmetic and copies ran while one was open for 23% of the time, Pallas kernels for 0%

commit v1 on v0

v1 whole, which is shorter than its diff:
```python
import functools

import jax
import jax.numpy as jnp
from jax import lax
from jax.experimental import pallas as pl
from jax.experimental.pallas import tpu as pltpu
from jax.sharding import PartitionSpec as P

BF, F32 = jnp.bfloat16, jnp.float32
MESH = pl.DeviceIdType.MESH
VMEM_LIMIT = 67_000_000
NT = (((1,), (1,)), ((), ()))


def normed(wide):
    scale = lax.rsqrt(jnp.mean(wide * wide, -1, keepdims=True) + 1e-6)
    return (wide * scale).astype(BF)


def dot(a, b):
    return jnp.dot(a, b, preferred_element_type=F32)


def dot_nt(a, b):
    return lax.dot_general(a, b, NT, preferred_element_type=F32)


class Place:
    def __init__(self, n):
        self.n, self.chips = n, n // 2
        self.me = lax.axis_index("dp")
        self.core = lax.rem(self.me, 2)
        self.chip = lax.div(self.me, 2)
        self.partner = self.chip * 2 + (1 - self.core)

    def at(self, offset):
        return lax.rem(self.chip + offset + self.chips, self.chips)

    def device(self, offset):
        return self.at(offset) * 2 + self.core


def greet(devices):
    barrier = pltpu.get_barrier_semaphore()
    for device in devices:
        pl.semaphore_signal(barrier, inc=1, device_id={"dp": device}, device_id_type=MESH)
    pl.semaphore_wait(barrier, len(devices))


def remote(src, dst, send, recv, device):
    return pltpu.make_async_remote_copy(
        src_ref=src, dst_ref=dst, send_sem=send, recv_sem=recv, device_id={"dp": device}, device_id_type=MESH
    )


class Gather:
    def __init__(self, place, shards, fulls, sems):
        self.p, self.shards, self.fulls = place, shards, fulls
        self.local, self.rs, self.rr, self.ps, self.pr = sems
        self.half_hops = place.chips // 2

    @staticmethod
    def sems(n, pieces):
        return [
            pltpu.SemaphoreType.DMA((pieces,)),
            pltpu.SemaphoreType.DMA((pieces, 2, n // 4)),
            pltpu.SemaphoreType.DMA((pieces, 2, n // 4)),
            pltpu.SemaphoreType.DMA((pieces, n // 2)),
            pltpu.SemaphoreType.DMA((pieces, n // 2)),
        ]

    def half(self, ref, h):
        rows, cols = ref.shape
        if cols > rows * 8:
            return ref.at[:, h * (cols // 2) : (h + 1) * (cols // 2)]
        return ref.at[h * (rows // 2) : (h + 1) * (rows // 2), :]

    def hop(self, i, way, t):
        p, full = self.p, self.fulls[i]
        behind = (1 - t) if way == 0 else (t - 1)
        ref = full.at[p.device(behind)]
        if t == self.half_hops:
            ref = self.half(ref, way)
        return remote(ref, ref, self.rs.at[i, way, t - 1], self.rr.at[i, way, t - 1], p.device(1 if way == 0 else -1))

    def landed(self, i, way, t):
        p, full = self.p, self.fulls[i]
        ref = full.at[p.device(-t if way == 0 else t)]
        if t == self.half_hops:
            ref = self.half(ref, way)
        return remote(ref, ref, self.rs.at[i, way, t - 1], self.rr.at[i, way, t - 1], p.device(1))

    def hand(self, i, k):
        p, full = self.p, self.fulls[i]
        offset = 0 if k == 0 else (-(k + 1) // 2 if k % 2 else k // 2)
        ref = full.at[p.device(offset)]
        return remote(ref, ref, self.ps.at[i, k], self.pr.at[i, k], p.partner)

    def handed(self, i, k):
        p, full = self.p, self.fulls[i]
        offset = 0 if k == 0 else (-(k + 1) // 2 if k % 2 else k // 2)
        ref = full.at[p.at(offset) * 2 + (1 - p.core)]
        return remote(ref, ref, self.ps.at[i, k], self.pr.at[i, k], p.partner)

    def begin(self):
        own = [pltpu.make_async_copy(s, f.at[self.p.me], self.local.at[i]) for i, (s, f) in enumerate(zip(self.shards, self.fulls))]
        for c in own:
            c.start()
        for i, c in enumerate(own):
            c.wait()
            self.hop(i, 0, 1).start()
            self.hop(i, 1, 1).start()
            self.hand(i, 0).start()

    def events(self):
        return [(t, i) for t in range(1, self.half_hops + 1) for i in range(len(self.fulls))]

    def forward(self, t, i):
        last = self.half_hops
        for way in range(2):
            self.landed(i, way, t).wait_recv()
            if t < last:
                self.hop(i, way, t + 1).start()
                self.hand(i, 2 * t - 1 + way).start()
        if t == last:
            self.hand(i, 2 * last - 1).start()

    def finish(self):
        for i in range(len(self.fulls)):
            for k in range(self.p.chips):
                self.handed(i, k).wait_recv()
        for i in range(len(self.fulls)):
            for k in range(self.p.chips):
                self.hand(i, k).wait_send()
            for way in range(2):
                for t in range(1, self.half_hops + 1):
                    self.hop(i, way, t).wait_send()


def gather_kernel(n, layer, wg, wu, wd, fg, fu, fd, *sems):
    p = Place(n)
    greet([p.device(1), p.device(-1), p.partner])
    g = Gather(p, [w.at[layer] for w in (wg, wu, wd)], [fg, fu, fd], sems)
    g.begin()
    for t, i in g.events():
        g.forward(t, i)
    g.finish()


def forward_kernel(n, layer, tile, x, wg, wu, wd, sg, su, sd, y, fg, fu, fd, *sems):
    p = Place(n)
    greet([p.device(1), p.device(-1), p.partner])
    g = Gather(p, [w.at[layer] for w in (sg, su, sd)], [fg, fu, fd], sems)
    g.begin()
    events = g.events()
    tiles = x.shape[0] // tile
    ff = wg.shape[1]
    width = 512

    def body(i, _):
        rows = pl.ds(pl.multiple_of(i * tile, tile), tile)
        h = x[rows, :]
        a = normed(h.astype(F32))
        out = None
        for c in range(0, ff, width):
            gate = dot(a, wg[:, c : c + width])
            up = dot(a, wu[:, c : c + width])
            hid = (gate * jax.nn.sigmoid(gate) * up).astype(BF)
            term = dot(hid, wd[c : c + width, :])
            out = term if out is None else out + term
        y[rows, :] = h + out.astype(BF)
        for k, (t, j) in enumerate(events):
            @pl.when(i == k)
            def _(t=t, j=j):
                g.forward(t, j)
        return 0

    lax.fori_loop(0, tiles, body, 0)
    for t, j in events[tiles:]:
        g.forward(t, j)
    g.finish()


class Scatter:
    def __init__(self, place, refs, sems):
        self.p = place
        self.g_gu, self.q_gu, self.s_gu, self.r_gu, self.g_wd, self.q_wd, self.s_wd, self.r_wd = refs
        self.ss_gu, self.sr_gu, self.ss_wd, self.sr_wd, self.ps, self.pr = sems

    @staticmethod
    def scratch(n, gu, wd):
        chips = n // 2
        return [
            pltpu.VMEM((chips, chips, 2) + gu, BF),
            pltpu.VMEM((chips, chips) + gu, BF),
            pltpu.VMEM((chips, 2, 4) + gu, BF),
            pltpu.VMEM((chips, 2, 4) + gu, BF),
            pltpu.VMEM((chips, 2) + wd, BF),
            pltpu.VMEM((chips,) + wd, BF),
            pltpu.VMEM((chips, 2) + wd, BF),
            pltpu.VMEM((chips, 2) + wd, BF),
            pltpu.SemaphoreType.DMA((chips, 2, 4)),
            pltpu.SemaphoreType.DMA((chips, 2, 4)),
            pltpu.SemaphoreType.DMA((chips, 2)),
            pltpu.SemaphoreType.DMA((chips, 2)),
            pltpu.SemaphoreType.DMA((chips, 2)),
            pltpu.SemaphoreType.DMA((chips, 2)),
        ]

    def owner(self, b):
        half = self.p.chips // 2
        return lax.div(b, 2) + half * lax.rem(b, 2)

    def pair(self, b):
        p = self.p
        return [
            remote(self.g_gu.at[b, :, 1 - p.core], self.q_gu.at[b], self.ps.at[b, 0], self.pr.at[b, 0], p.partner),
            remote(self.g_wd.at[b, 1 - p.core], self.q_wd.at[b], self.ps.at[b, 1], self.pr.at[b, 1], p.partner),
        ]

    def own_gu(self, b, chip, cols):
        return self.g_gu[b, chip, self.p.core, :, cols].astype(F32) + self.q_gu[b, chip, :, cols].astype(F32)

    def own_wd(self, b, rows):
        return self.g_wd[b, self.p.core, rows, :].astype(F32) + self.q_wd[b, rows, :].astype(F32)

    def gu_copy(self, b, way, s):
        src, dst = self.s_gu.at[b, way, s], self.r_gu.at[b, way, s]
        if s == 0:
            w = src.shape[1] // 2
            src, dst = (r.at[:, way * w : (way + 1) * w] for r in (src, dst))
        return remote(src, dst, self.ss_gu.at[b, way, s], self.sr_gu.at[b, way, s], self.p.device(1 if way == 0 else -1))

    def wd_copy(self, b, way, first):
        src, dst = self.s_wd.at[b, way], self.r_wd.at[b, way]
        if first:
            h = src.shape[0] // 2
            src, dst = (r.at[way * h : (way + 1) * h, :] for r in (src, dst))
        return remote(src, dst, self.ss_wd.at[b, way], self.sr_wd.at[b, way], self.p.device(1 if way == 0 else -1))

    def stage(self, b, s):
        p = self.p
        if s == 0:
            for c in self.pair(b):
                c.wait_recv()
        width, height = self.g_gu.shape[-1] // 2, self.g_wd.shape[-2] // 2
        for way in range(2):
            far = 4 - s
            chip = p.at(far if way == 0 else -far)
            if s > 0:
                self.gu_copy(b, way, s - 1).wait_recv()
            for h in range(2):
                cols = slice(h * width, (h + 1) * width)
                if s == 0 and h != way:
                    continue
                term = self.own_gu(b, chip, cols)
                if s > 1 or (s == 1 and h == way):
                    term = term + self.r_gu[b, way, s - 1, :, cols].astype(F32)
                self.s_gu[b, way, s, :, cols] = term.astype(BF)
            self.gu_copy(b, way, s).start()

        owner = self.owner(b)
        for way in range(2):
            far = 4 - s

            @pl.when(owner == p.at(far if way == 0 else -far))
            def _(way=way):
                if s > 0:
                    self.wd_copy(b, way, s == 1).wait_recv()
                for h in range(2):
                    rows = slice(h * height, (h + 1) * height)
                    if s == 0 and h != way:
                        continue
                    term = self.own_wd(b, rows)
                    if s > 1 or (s == 1 and h == way):
                        term = term + self.r_wd[b, way, rows, :].astype(F32)
                    self.s_wd[b, way, rows, :] = term.astype(BF)
                self.wd_copy(b, way, s == 0).start()

    def last(self, b, out_gu, out_wd):
        p = self.p
        owner = self.owner(b)
        full = slice(None)
        width = self.g_gu.shape[-1]
        for way in range(2):
            self.gu_copy(b, way, 3).wait_recv()
        total = self.own_gu(b, p.chip, full) + self.r_gu[b, 0, 3].astype(F32) + self.r_gu[b, 1, 3].astype(F32)
        out_gu[:, pl.ds(pl.multiple_of(owner * width, width), width)] = total.astype(BF)

        @pl.when(owner == p.chip)
        def _():
            for way in range(2):
                self.wd_copy(b, way, False).wait_recv()
            out_wd[...] = (self.own_wd(b, full) + self.r_wd[b, 0].astype(F32) + self.r_wd[b, 1].astype(F32)).astype(BF)

    def drain(self):
        p = self.p

        def body(b, _):
            for c in self.pair(b):
                c.wait_send()
            owner = self.owner(b)
            for way in range(2):
                for s in range(4):
                    self.gu_copy(b, way, s).wait_send()
                    far = 4 - s

                    @pl.when(owner == p.at(far if way == 0 else -far))
                    def _(way=way, s=s):
                        self.wd_copy(b, way, s == 0).wait_send()
            return 0

        lax.fori_loop(0, p.chips, body, 0)


def backward_kernel(n, tile, final, *refs):
    refs = list(refs)
    take = lambda k: [refs.pop(0) for _ in range(k)]
    h, dy, wg, wu, wd = take(5)
    before = take(2) if final else []
    out_gu, out_wd, out = take(3)
    a, at, dyt, hid, dgate, dup = take(6)
    if not final:
        dag, dau = take(2)
    else:
        mine, theirs, sq_send, sq_recv = take(4)
    p = Place(n)
    if final:
        greet([lax.rem(p.me + k, n) for k in range(1, n)])
    else:
        greet([p.device(1), p.device(-1), p.partner])
    sc = Scatter(p, take(8), take(6))
    tokens, d = h.shape
    block = hid.shape[1]
    blocks = p.chips

    def prepare(i, _):
        rows = pl.ds(pl.multiple_of(i * 256, 256), 256)
        one = normed(h[rows, :].astype(F32))
        a[rows, :] = one
        at[:, rows] = one.T
        dyt[:, rows] = dy[rows, :].T
        if not final:
            dag[rows, :] = jnp.zeros((256, d), F32)
            dau[rows, :] = jnp.zeros((256, d), F32)
        return 0

    lax.fori_loop(0, tokens // 256, prepare, 0)

    def step(b, _):
        owner = sc.owner(b)

        @pl.when(b < blocks)
        def _():
            cols = pl.ds(pl.multiple_of(owner * block, block), block)

            def part(i, _):
                rows = pl.ds(pl.multiple_of(i * tile, tile), tile)
                one = a[rows, :]
                gate = dot(one, wg[:, cols])
                up = dot(one, wu[:, cols])
                by_hid = dot_nt(dy[rows, :], wd[cols, :]).astype(BF).astype(F32)
                s = jax.nn.sigmoid(gate)
                t = gate * s
                hid[rows, :] = (t * up).astype(BF)
                by_up = (t * by_hid).astype(BF)
                by_t = by_hid * up
                by_gate = (by_t * s + gate * by_t * (s * (1.0 - s))).astype(BF)
                dup[rows, :] = by_up
                dgate[rows, :] = by_gate
                if not final:
                    dag[rows, :] += dot_nt(by_gate, wg[:, cols])
                    dau[rows, :] += dot_nt(by_up, wu[:, cols])
                return 0

            lax.fori_loop(0, tokens // tile, part, 0)

        for s in range(4):
            @pl.when((b - 1 - s >= 0) & (b - 1 - s < blocks))
            def _(s=s):
                sc.stage(b - 1 - s, s)

        @pl.when((b - 5 >= 0) & (b - 5 < blocks))
        def _():
            sc.last(b - 5, out_gu, out_wd)

        @pl.when(b < blocks)
        def _():
            for_gate = dot(at[...], dgate[...])
            for_up = dot(at[...], dup[...])
            each = d // n
            for k in range(n):
                rows = slice(k * each, (k + 1) * each)
                sc.g_gu[b, k // 2, k % 2] = jnp.concatenate([for_gate[rows], for_up[rows]], 0).astype(BF)
            for_down = dot(dyt[...], hid[...]).T.astype(BF)
            sc.g_wd[b, 0] = for_down[: block // 2]
            sc.g_wd[b, 1] = for_down[block // 2 :]
            for c in sc.pair(b):
                c.start()

        return 0

    lax.fori_loop(0, blocks + 5, step, 0)

    if final:
        total = jnp.zeros((1, 1), F32)
        for ref in (out_gu, out_wd, *before):
            one = ref[...].astype(F32)
            total = total + jnp.sum(jnp.sum(one * one, axis=1, keepdims=True), axis=0, keepdims=True)
        mine[...] = jnp.broadcast_to(total, mine.shape)

        def to(k):
            return remote(mine, theirs.at[k - 1], sq_send.at[k - 1], sq_recv.at[k - 1], lax.rem(p.me + k, n))

        for k in range(1, n):
            to(k).start()
        for k in range(1, n):
            to(k).wait_recv()
        acc = mine[...]
        for k in range(1, n):
            acc = acc + theirs[k - 1]
        out[...] = acc
        for k in range(1, n):
            to(k).wait_send()
    else:
        def close(i, _):
            rows = pl.ds(pl.multiple_of(i * 256, 256), 256)
            wide = h[rows, :].astype(F32)
            mean = jnp.mean(wide * wide, -1, keepdims=True) + 1e-6
            scale = lax.rsqrt(mean)
            by_a = (dag[rows, :].astype(BF) + dau[rows, :].astype(BF)).astype(F32)
            inner = jnp.sum(wide * by_a, -1, keepdims=True)
            by_h = by_a * scale + (inner * (-0.5 * scale / mean) / d) * (2.0 * wide)
            out[rows, :] = dy[rows, :] + by_h.astype(BF)
            return 0

        lax.fori_loop(0, tokens // 256, close, 0)
    sc.drain()


def adamw(w, m, v, g):
    m = 0.9 * m + 0.1 * g
    v = 0.95 * v + 0.05 * g * g
    step = m * lax.rsqrt(v + 1e-8) + 0.1 * w
    return (w - 0.02 * step).astype(BF), m, v


def solution(mesh):
    n = mesh.shape["dp"]
    any_, vmem = pl.BlockSpec(memory_space=pl.ANY), pl.BlockSpec(memory_space=pltpu.VMEM)

    def params(k):
        return pltpu.CompilerParams(collective_id=k, has_side_effects=True, vmem_limit_bytes=VMEM_LIMIT)

    def shape(*s, dtype=BF):
        return jax.ShapeDtypeStruct(s, dtype)

    def step(x, dy, *arrays):
        weights, m, v = (arrays[i : i + 3] for i in (0, 3, 6))
        wg, wu, wd = weights
        x, dy = x[0], dy[0]
        tokens, d = x.shape
        rows, ff = wg.shape[1:]
        deep = wd.shape[1]
        fulls = [shape(n, rows, ff), shape(n, rows, ff), shape(n, deep, d)]
        flat = lambda f: (f[0].reshape(d, ff), f[1].reshape(d, ff), f[2].reshape(ff, d))
        first = pl.pallas_call(
            functools.partial(gather_kernel, n, 0),
            out_shape=fulls,
            in_specs=[any_] * 3,
            out_specs=[vmem] * 3,
            scratch_shapes=Gather.sems(n, 3),
            compiler_params=params(0),
            name="gather0",
        )(wg, wu, wd)
        w0 = flat(first)
        h, *second = pl.pallas_call(
            functools.partial(forward_kernel, n, 1, 256),
            out_shape=[shape(tokens, d)] + fulls,
            in_specs=[vmem] * 4 + [any_] * 3,
            out_specs=[vmem] * 4,
            scratch_shapes=Gather.sems(n, 3),
            compiler_params=params(1),
            name="forward0",
        )(x, *w0, wg, wu, wd)
        w1 = flat(second)

        block = ff // (n // 2)
        gu, wdb = (2 * rows, block), (deep, d)
        common = [
            pltpu.VMEM((tokens, d), BF),
            pltpu.VMEM((d, tokens), BF),
            pltpu.VMEM((d, tokens), BF),
            pltpu.VMEM((tokens, block), BF),
            pltpu.VMEM((tokens, block), BF),
            pltpu.VMEM((tokens, block), BF),
        ]
        gu1, wd1, dh = pl.pallas_call(
            functools.partial(backward_kernel, n, 512, False),
            out_shape=[shape(2 * rows, ff), shape(deep, d), shape(tokens, d)],
            in_specs=[vmem] * 5,
            out_specs=[vmem] * 3,
            scratch_shapes=common + [pltpu.VMEM((tokens, d), F32)] * 2 + Scatter.scratch(n, gu, wdb),
            compiler_params=params(2),
            name="backward1",
        )(h, dy, *w1)
        gu0, wd0, squares = pl.pallas_call(
            functools.partial(backward_kernel, n, 512, True),
            out_shape=[shape(2 * rows, ff), shape(deep, d), shape(8, 128, dtype=F32)],
            in_specs=[vmem] * 7,
            out_specs=[vmem] * 3,
            scratch_shapes=common
            + [
                pltpu.VMEM((8, 128), F32),
                pltpu.VMEM((n - 1, 8, 128), F32),
                pltpu.SemaphoreType.DMA((n - 1,)),
                pltpu.SemaphoreType.DMA((n - 1,)),
            ]
            + Scatter.scratch(n, gu, wdb),
            compiler_params=params(3),
            name="backward0",
        )(x, dh, *w0, gu1, wd1)

        gradients = [
            jnp.stack([gu0[:rows], gu1[:rows]]),
            jnp.stack([gu0[rows:], gu1[rows:]]),
            jnp.stack([wd0, wd1]),
        ]
        count = n * sum(g.size for g in gradients)
        factor = jnp.minimum(1.0, 0.5 * lax.rsqrt(squares[0, 0] / count + 1e-30))
        new = [adamw(w.astype(F32), m, v, g.astype(F32) * factor) for w, m, v, g in zip(weights, m, v, gradients, strict=True)]
        return tuple(one[which] for which in range(3) for one in new)

    states, cut = P(("rep", "dp"), None, None), P(None, "dp", None)
    return jax.shard_map(
        step,
        mesh=mesh,
        in_specs=(states, states) + (cut,) * 9,
        out_specs=(P("rep", "dp", None),) * 9,
        check_vma=False,
    )
```

time: 692 us -> 325 us (0.47); the launches traced: 684 us -> 325 us
  waiting for transfers between devices: 412 us -> 0 us
  Pallas kernels: 0 us -> 315 us
  matrix products: 195 us -> 0 us
  blocking collectives: 27.1 us -> 0 us
  between operations: 17.5 us -> 1.45 us
  local copies, waits for them, and re-layouts: 17.9 us -> 3.42 us
  other arithmetic: 14 us -> 4.97 us
    pallas_call x0 -> x4, Pallas kernels: none -> 315 us  [the longest x1 108 us: step(): pl.pallas_call(functools.partial(backward_kernel, n, 512, False), out_sha...]
    reduce_scatter x6 -> x0, waiting for transfers between devices: 258 us -> none  [step(): lax.psum_scatter(by_w[name], 'dp', scatter_dimension=0, tiled=True)]
    dot_general x15 -> x0, matrix products: 195 us -> none  [the longest x5 71.5 us: layer(): gate = jnp.dot(a, w['w_gate'], preferred_element_type=jnp.float32)]
    all_gather x6 -> x0, waiting for transfers between devices: 152 us -> none  [fetched(): lax.all_gather(w[number], 'dp', axis=0, tiled=True)]
    psum x1 -> x0, blocking collectives: 27.1 us -> none  [step(): squares = lax.psum(sum((jnp.sum(g * g) for g in gradients)), 'dp')]
    unnamed x36 -> x12, local copies, waits for them, and re-layouts: 12.6 us -> 0.04 us
  transfers between devices with their start and end apart: 12 -> 0, of which waited for: 11 -> 0; matrix products, arithmetic and copies ran while one was open for 23% -> 0% of each run, Pallas kernels for 0% -> 0%
where the time goes in v1:
time: 325 us
  Pallas kernels  315 us (97%)
  other arithmetic  4.97 us (2%)
  local copies, waits for them, and re-layouts  3.42 us (1%)
    pallas_call x1, Pallas kernels, step(): pl.pallas_call(functools.partial(backward_kernel, n, 512, False), out_sha...  108 us
    pallas_call x1, Pallas kernels, step(): pl.pallas_call(functools.partial(backward_kernel, n, 512, True), out_shap...  102 us
    pallas_call x1, Pallas kernels, step(): pl.pallas_call(functools.partial(gather_kernel, n, 0), out_shape=fulls, i...  52.8 us
    pallas_call x1, Pallas kernels, step(): pl.pallas_call(functools.partial(forward_kernel, n, 1, 256), out_shape=[s...  51.9 us

profile of v1, /device:TPU:21, one launch (start us, length us, event | category | flops | bytes accessed | tf_op | source)
XLA Modules:
  0.0 324.8 jit_solution(5224358933833648101)
XLA Ops:
  0.6 52.8 %gather0.1 = (bf16[16,40,2048]{2,1,0:T(8,128)(2,1)}, bf16[16,40,2048]{2,1,0:T(8,128)(2,1)}, bf16[16,128,640]{2,1,0:T(8,128)(2,1)}) custom-call(bf16[2,40,2048]{2,1,0:T(8,128)(2,1)} %sg.1, bf16[2,40,2048]{2,1,0:T(8,128)(2,1)} %su.1, bf16[2,128,640]{2,1,0:T(8,128)(2,1)} %sd.1), custom_call_target="tpu_custom_call" | custom-call | tf_op jit(solution)/shard_map/gather0/pallas_call | solution.py:468
  53.5 51.9 %forward0.1 = (bf16[2048,640]{1,0:T(8,128)(2,1)}, bf16[16,40,2048]{2,1,0:T(8,128)(2,1)}, bf16[16,40,2048]{2,1,0:T(8,128)(2,1)}, bf16[16,128,640]{2,1,0:T(8,128)(2,1)}) custom-call(bf16[2048,640]{1,0:T(8,128)(2,1)} %bitcast.19, bf16[640,2048]{1,0:T(8,128)(2,1)} %bitcast.21, bf16[640,2048]{1,0:T(8,128)(2,1)} %bitcast.23, bf16[2048,640]{1,0:T(8,128)(2,1)} %bitcast.25, ...), custom_call_target="tpu_custom_call" | custom-call | tf_op jit(solution)/shard_map/forward0/pallas_call | solution.py:478
  105.4 108.3 %backward1.1 = (bf16[80,2048]{1,0:T(8,128)(2,1)}, bf16[128,640]{1,0:T(8,128)(2,1)}, bf16[2048,640]{1,0:T(8,128)(2,1)}) custom-call(bf16[2048,640]{1,0:T(8,128)(2,1)} %get-tuple-element.25.refs_0_, bf16[2048,640]{1,0:T(8,128)(2,1)} %bitcast.27, bf16[640,2048]{1,0:T(8,128)(2,1)} %bitcast.28, bf16[640,2048]{1,0:T(8,128)(2,1)} %bitcast.29, ...), custom_call_target="tpu_custom_call" | custom-call | tf_op jit(solution)/shard_map/backward1/pallas_call | solution.py:499
  213.7 101.9 %backward0.1 = (bf16[80,2048]{1,0:T(8,128)(2,1)}, bf16[128,640]{1,0:T(8,128)(2,1)}, f32[8,128]{1,0:T(8,128)}) custom-call(bf16[2048,640]{1,0:T(8,128)(2,1)} %bitcast.20, bf16[2048,640]{1,0:T(8,128)(2,1)} %get-tuple-element.29.refs_1_, bf16[640,2048]{1,0:T(8,128)(2,1)} %bitcast.22, bf16[640,2048]{1,0:T(8,128)(2,1)} %bitcast.24, bf16[2048,640]{1,0:T(8,128)(2,1)} %bitcast.26, ...), custom_call_target="tpu_custom_call" | custom-call | tf_op jit(solution)/shard_map/backward0/pallas_call | solution.py:508
  315.6 0.0 copy-start
  315.6 0.0 copy-start.1
  315.7 0.0 copy-start.2
  315.7 0.0 copy-start.3
  315.7 0.0 copy-start.4
  315.7 0.0 copy-start.5
  315.7 1.3 slice.17
  317.8 1.0 slice_bitcast_fusion.1
  318.8 1.0 slice_bitcast_fusion
  319.8 2.9 fusion.8
  322.6 0.0 copy-done
  322.7 0.0 copy-done.1
  322.7 0.0 copy-done.2
  322.7 0.0 copy-done.3
  322.7 0.0 copy-done.4
  322.7 0.0 copy-done.5
  322.7 2.1 fusion.2
Async XLA Ops:
  315.6 7.0 %copy-start = (bf16[2,40,2048]{2,1,0:T(8,128)(2,1)S(1)}, bf16[2,40,2048]{2,1,0:T(8,128)(2,1)}, u32[]{:S(2)}) copy-start(bf16[2,40,2048]{2,1,0:T(8,128)(2,1)} %sg.1) | copy-start | bytes 983044
  315.6 7.0 %copy-start.1 = (bf16[2,40,2048]{2,1,0:T(8,128)(2,1)S(1)}, bf16[2,40,2048]{2,1,0:T(8,128)(2,1)}, u32[]{:S(2)}) copy-start(bf16[2,40,2048]{2,1,0:T(8,128)(2,1)} %su.1) | copy-start | bytes 983044
  315.7 7.0 %copy-start.2 = (f32[2,40,2048]{2,1,0:T(8,128)S(1)}, f32[2,40,2048]{2,1,0:T(8,128)}, u32[]{:S(2)}) copy-start(f32[2,40,2048]{2,1,0:T(8,128)} %param.19) | copy-start | bytes 1966084
  315.7 7.0 %copy-start.3 = (f32[2,40,2048]{2,1,0:T(8,128)S(1)}, f32[2,40,2048]{2,1,0:T(8,128)}, u32[]{:S(2)}) copy-start(f32[2,40,2048]{2,1,0:T(8,128)} %param.16) | copy-start | bytes 1966084
  315.7 7.0 %copy-start.4 = (f32[2,40,2048]{2,1,0:T(8,128)S(1)}, f32[2,40,2048]{2,1,0:T(8,128)}, u32[]{:S(2)}) copy-start(f32[2,40,2048]{2,1,0:T(8,128)} %param.20) | copy-start | bytes 1966084
  315.7 7.0 %copy-start.5 = (f32[2,40,2048]{2,1,0:T(8,128)S(1)}, f32[2,40,2048]{2,1,0:T(8,128)}, u32[]{:S(2)}) copy-start(f32[2,40,2048]{2,1,0:T(8,128)} %param.17) | copy-start | bytes 1966084

commit v2 on v1

--- a/solution.py
+++ b/solution.py
@@ -210,6 +210,7 @@
 
     def owner(self, b):
         half = self.p.chips // 2
+        b = lax.rem(b, self.p.chips)
         return lax.div(b, 2) + half * lax.rem(b, 2)
 
     def pair(self, b):
@@ -239,8 +240,9 @@
             src, dst = (r.at[way * h : (way + 1) * h, :] for r in (src, dst))
         return remote(src, dst, self.ss_wd.at[b, way], self.sr_wd.at[b, way], self.p.device(1 if way == 0 else -1))
 
-    def stage(self, b, s):
+    def stage(self, chain, s):
         p = self.p
+        b = lax.rem(chain, p.chips)
         if s == 0:
             for c in self.pair(b):
                 c.wait_recv()
@@ -278,165 +280,208 @@
                     self.s_wd[b, way, rows, :] = term.astype(BF)
                 self.wd_copy(b, way, s == 0).start()
 
-    def last(self, b, out_gu, out_wd):
+    def last(self, chain, out_gate, out_up, out_wd):
         p = self.p
+        b = lax.rem(chain, p.chips)
+        layer = out_wd.shape[0] - 1 - lax.div(chain, p.chips)
         owner = self.owner(b)
         full = slice(None)
         width = self.g_gu.shape[-1]
+        rows = self.g_gu.shape[-2] // 2
         for way in range(2):
             self.gu_copy(b, way, 3).wait_recv()
         total = self.own_gu(b, p.chip, full) + self.r_gu[b, 0, 3].astype(F32) + self.r_gu[b, 1, 3].astype(F32)
-        out_gu[:, pl.ds(pl.multiple_of(owner * width, width), width)] = total.astype(BF)
+        cols = pl.ds(pl.multiple_of(owner * width, width), width)
+        out_gate[layer, :, cols] = total[:rows].astype(BF)
+        out_up[layer, :, cols] = total[rows:].astype(BF)
 
         @pl.when(owner == p.chip)
         def _():
             for way in range(2):
                 self.wd_copy(b, way, False).wait_recv()
-            out_wd[...] = (self.own_wd(b, full) + self.r_wd[b, 0].astype(F32) + self.r_wd[b, 1].astype(F32)).astype(BF)
-
-    def drain(self):
+            out_wd[layer] = (self.own_wd(b, full) + self.r_wd[b, 0].astype(F32) + self.r_wd[b, 1].astype(F32)).astype(BF)
+
+    def drain(self, chain):
         p = self.p
-
-        def body(b, _):
-            for c in self.pair(b):
-                c.wait_send()
-            owner = self.owner(b)
-            for way in range(2):
-                for s in range(4):
-                    self.gu_copy(b, way, s).wait_send()
-                    far = 4 - s
-
-                    @pl.when(owner == p.at(far if way == 0 else -far))
-                    def _(way=way, s=s):
-                        self.wd_copy(b, way, s == 0).wait_send()
-            return 0
-
-        lax.fori_loop(0, p.chips, body, 0)
-
-
-def backward_kernel(n, tile, final, *refs):
+        b = lax.rem(chain, p.chips)
+        for c in self.pair(b):
+            c.wait_send()
+        owner = self.owner(b)
+        for way in range(2):
+            for s in range(4):
+                self.gu_copy(b, way, s).wait_send()
+                far = 4 - s
+
+                @pl.when(owner == p.at(far if way == 0 else -far))
+                def _(way=way, s=s):
+                    self.wd_copy(b, way, s == 0).wait_send()
+
+
+def backward_kernel(n, tile, x, h, dy, wg0, wu0, wd0, wg1, wu1, wd1, out_gate, out_up, out_wd, out, *refs):
     refs = list(refs)
     take = lambda k: [refs.pop(0) for _ in range(k)]
-    h, dy, wg, wu, wd = take(5)
-    before = take(2) if final else []
-    out_gu, out_wd, out = take(3)
-    a, at, dyt, hid, dgate, dup = take(6)
-    if not final:
-        dag, dau = take(2)
-    else:
-        mine, theirs, sq_send, sq_recv = take(4)
+    hs, by, a, at, dyt, hid, dgate, dup, dag, dau, bg, bu, bd, mine, theirs = take(15)
+    in_sem, w_sem, sq_send, sq_recv = take(4)
     p = Place(n)
-    if final:
-        greet([lax.rem(p.me + k, n) for k in range(1, n)])
-    else:
-        greet([p.device(1), p.device(-1), p.partner])
     sc = Scatter(p, take(8), take(6))
-    tokens, d = h.shape
+    tokens, d = by.shape
     block = hid.shape[1]
     blocks = p.chips
+    chains = 2 * blocks
+    step_rows = 256
+
+    loads = [
+        pltpu.make_async_copy(h, hs.at[1], in_sem.at[0]),
+        pltpu.make_async_copy(dy, by, in_sem.at[1]),
+        pltpu.make_async_copy(x, hs.at[0], in_sem.at[2]),
+    ]
+
+    def fetch(b, weights):
+        cols = pl.ds(pl.multiple_of(sc.owner(b) * block, block), block)
+        slot = lax.rem(b, 2)
+        g, u, w = weights
+        return [
+            pltpu.make_async_copy(g.at[:, cols], bg.at[slot], w_sem.at[slot, 0]),
+            pltpu.make_async_copy(u.at[:, cols], bu.at[slot], w_sem.at[slot, 1]),
+            pltpu.make_async_copy(w.at[cols, :], bd.at[slot], w_sem.at[slot, 2]),
+        ]
+
+    first, second = (wg1, wu1, wd1), (wg0, wu0, wd0)
+    for c in loads + fetch(0, first):
+        c.start()
+    greet([lax.rem(p.me + k, n) for k in range(1, n)])
+    for c in loads[:2]:
+        c.wait()
 
     def prepare(i, _):
-        rows = pl.ds(pl.multiple_of(i * 256, 256), 256)
-        one = normed(h[rows, :].astype(F32))
+        rows = pl.ds(pl.multiple_of(i * step_rows, step_rows), step_rows)
+        one = normed(hs[1, rows, :].astype(F32))
         a[rows, :] = one
         at[:, rows] = one.T
-        dyt[:, rows] = dy[rows, :].T
-        if not final:
-            dag[rows, :] = jnp.zeros((256, d), F32)
-            dau[rows, :] = jnp.zeros((256, d), F32)
+        dyt[:, rows] = by[rows, :].T
+        dag[rows, :] = jnp.zeros((step_rows, d), F32)
+        dau[rows, :] = jnp.zeros((step_rows, d), F32)
         return 0
 
-    lax.fori_loop(0, tokens // 256, prepare, 0)
+    lax.fori_loop(0, tokens // step_rows, prepare, 0)
+
+    def turn(i, _):
+        rows = pl.ds(pl.multiple_of(i * step_rows, step_rows), step_rows)
+        wide = hs[1, rows, :].astype(F32)
+        mean = jnp.mean(wide * wide, -1, keepdims=True) + 1e-6
+        scale = lax.rsqrt(mean)
+        by_a = (dag[rows, :].astype(BF) + dau[rows, :].astype(BF)).astype(F32)
+        inner = jnp.sum(wide * by_a, -1, keepdims=True)
+        by_h = by_a * scale + (inner * (-0.5 * scale / mean) / d) * (2.0 * wide)
+        new = by[rows, :] + by_h.astype(BF)
+        by[rows, :] = new
+        dyt[:, rows] = new.T
+        one = normed(hs[0, rows, :].astype(F32))
+        a[rows, :] = one
+        at[:, rows] = one.T
+        return 0
+
+    def part(slot, with_da, i, _):
+        rows = pl.ds(pl.multiple_of(i * tile, tile), tile)
+        one = a[rows, :]
+        gate = dot(one, bg[slot])
+        up = dot(one, bu[slot])
+        by_hid = dot_nt(by[rows, :], bd[slot]).astype(BF).astype(F32)
+        s = jax.nn.sigmoid(gate)
+        t = gate * s
+        hid[rows, :] = (t * up).astype(BF)
+        by_up = (t * by_hid).astype(BF)
+        by_t = by_hid * up
+        by_gate = (by_t * s + gate * by_t * (s * (1.0 - s))).astype(BF)
+        dup[rows, :] = by_up
+        dgate[rows, :] = by_gate
+        if with_da:
+            dag[rows, :] += dot_nt(by_gate, bg[slot])
+            dau[rows, :] += dot_nt(by_up, bu[slot])
+        return 0
 
     def step(b, _):
-        owner = sc.owner(b)
+        slot = lax.rem(b, 2)
+
+        @pl.when(b < blocks - 1)
+        def _():
+            for c in fetch(b + 1, first):
+                c.start()
+
+        @pl.when((b >= blocks - 1) & (b < chains - 1))
+        def _():
+            for c in fetch(b + 1, second):
+                c.start()
+
+        @pl.when(b == blocks)
+        def _():
+            loads[2].wait()
+            lax.fori_loop(0, tokens // step_rows, turn, 0)
 
         @pl.when(b < blocks)
         def _():
-            cols = pl.ds(pl.multiple_of(owner * block, block), block)
-
-            def part(i, _):
-                rows = pl.ds(pl.multiple_of(i * tile, tile), tile)
-                one = a[rows, :]
-                gate = dot(one, wg[:, cols])
-                up = dot(one, wu[:, cols])
-                by_hid = dot_nt(dy[rows, :], wd[cols, :]).astype(BF).astype(F32)
-                s = jax.nn.sigmoid(gate)
-                t = gate * s
-                hid[rows, :] = (t * up).astype(BF)
-                by_up = (t * by_hid).astype(BF)
-                by_t = by_hid * up
-                by_gate = (by_t * s + gate * by_t * (s * (1.0 - s))).astype(BF)
-                dup[rows, :] = by_up
-                dgate[rows, :] = by_gate
-                if not final:
-                    dag[rows, :] += dot_nt(by_gate, wg[:, cols])
-                    dau[rows, :] += dot_nt(by_up, wu[:, cols])
-                return 0
-
-            lax.fori_loop(0, tokens // tile, part, 0)
+            for c in fetch(b, first):
+                c.wait()
+            lax.fori_loop(0, tokens // tile, functools.partial(part, slot, True), 0)
+
+        @pl.when((b >= blocks) & (b < chains))
+        def _():
+            for c in fetch(b, second):
+                c.wait()
+            lax.fori_loop(0, tokens // tile, functools.partial(part, slot, False), 0)
 
         for s in range(4):
-            @pl.when((b - 1 - s >= 0) & (b - 1 - s < blocks))
+            @pl.when((b - 1 - s >= 0) & (b - 1 - s < chains))
             def _(s=s):
                 sc.stage(b - 1 - s, s)
 
-        @pl.when((b - 5 >= 0) & (b - 5 < blocks))
-        def _():
-            sc.last(b - 5, out_gu, out_wd)
-
-        @pl.when(b < blocks)
-        def _():
+        @pl.when((b - 5 >= 0) & (b - 5 < chains))
+        def _():
+            sc.last(b - 5, out_gate, out_up, out_wd)
+
+        @pl.when((b - 6 >= 0) & (b - 6 < chains))
+        def _():
+            sc.drain(b - 6)
+
+        @pl.when(b < chains)
+        def _():
+            q = lax.rem(b, blocks)
             for_gate = dot(at[...], dgate[...])
             for_up = dot(at[...], dup[...])
             each = d // n
             for k in range(n):
                 rows = slice(k * each, (k + 1) * each)
-                sc.g_gu[b, k // 2, k % 2] = jnp.concatenate([for_gate[rows], for_up[rows]], 0).astype(BF)
+                sc.g_gu[q, k // 2, k % 2] = jnp.concatenate([for_gate[rows], for_up[rows]], 0).astype(BF)
             for_down = dot(dyt[...], hid[...]).T.astype(BF)
-            sc.g_wd[b, 0] = for_down[: block // 2]
-            sc.g_wd[b, 1] = for_down[block // 2 :]
-            for c in sc.pair(b):
+            sc.g_wd[q, 0] = for_down[: block // 2]
+            sc.g_wd[q, 1] = for_down[block // 2 :]
+            for c in sc.pair(q):
                 c.start()
 
         return 0
 
-    lax.fori_loop(0, blocks + 5, step, 0)
-
-    if final:
-        total = jnp.zeros((1, 1), F32)
-        for ref in (out_gu, out_wd, *before):
-            one = ref[...].astype(F32)
+    lax.fori_loop(0, chains + 6, step, 0)
+
+    total = jnp.zeros((1, 1), F32)
+    for ref in (out_gate, out_up, out_wd):
+        for k in range(2):
+            one = ref[k].astype(F32)
             total = total + jnp.sum(jnp.sum(one * one, axis=1, keepdims=True), axis=0, keepdims=True)
-        mine[...] = jnp.broadcast_to(total, mine.shape)
-
-        def to(k):
-            return remote(mine, theirs.at[k - 1], sq_send.at[k - 1], sq_recv.at[k - 1], lax.rem(p.me + k, n))
-
-        for k in range(1, n):
-            to(k).start()
-        for k in range(1, n):
-            to(k).wait_recv()
-        acc = mine[...]
-        for k in range(1, n):
-            acc = acc + theirs[k - 1]
-        out[...] = acc
-        for k in range(1, n):
-            to(k).wait_send()
-    else:
-        def close(i, _):
-            rows = pl.ds(pl.multiple_of(i * 256, 256), 256)
-            wide = h[rows, :].astype(F32)
-            mean = jnp.mean(wide * wide, -1, keepdims=True) + 1e-6
-            scale = lax.rsqrt(mean)
-            by_a = (dag[rows, :].astype(BF) + dau[rows, :].astype(BF)).astype(F32)
-            inner = jnp.sum(wide * by_a, -1, keepdims=True)
-            by_h = by_a * scale + (inner * (-0.5 * scale / mean) / d) * (2.0 * wide)
-            out[rows, :] = dy[rows, :] + by_h.astype(BF)
-            return 0
-
-        lax.fori_loop(0, tokens // 256, close, 0)
-    sc.drain()
+    mine[...] = jnp.broadcast_to(total, mine.shape)
+
+    def to(k):
+        return remote(mine, theirs.at[k - 1], sq_send.at[k - 1], sq_recv.at[k - 1], lax.rem(p.me + k, n))
+
+    for k in range(1, n):
+        to(k).start()
+    for k in range(1, n):
+        to(k).wait_recv()
+    acc = mine[...]
+    for k in range(1, n):
+        acc = acc + theirs[k - 1]
+    out[...] = acc
+    for k in range(1, n):
+        to(k).wait_send()
 
 
 def adamw(w, m, v, g):
@@ -487,46 +532,37 @@
         w1 = flat(second)
 
         block = ff // (n // 2)
-        gu, wdb = (2 * rows, block), (deep, d)
-        common = [
-            pltpu.VMEM((tokens, d), BF),
-            pltpu.VMEM((d, tokens), BF),
-            pltpu.VMEM((d, tokens), BF),
-            pltpu.VMEM((tokens, block), BF),
-            pltpu.VMEM((tokens, block), BF),
-            pltpu.VMEM((tokens, block), BF),
-        ]
-        gu1, wd1, dh = pl.pallas_call(
-            functools.partial(backward_kernel, n, 512, False),
-            out_shape=[shape(2 * rows, ff), shape(deep, d), shape(tokens, d)],
-            in_specs=[vmem] * 5,
-            out_specs=[vmem] * 3,
-            scratch_shapes=common + [pltpu.VMEM((tokens, d), F32)] * 2 + Scatter.scratch(n, gu, wdb),
-            compiler_params=params(2),
-            name="backward1",
-        )(h, dy, *w1)
-        gu0, wd0, squares = pl.pallas_call(
-            functools.partial(backward_kernel, n, 512, True),
-            out_shape=[shape(2 * rows, ff), shape(deep, d), shape(8, 128, dtype=F32)],
-            in_specs=[vmem] * 7,
-            out_specs=[vmem] * 3,
-            scratch_shapes=common
-            + [
+        *gradients, squares = pl.pallas_call(
+            functools.partial(backward_kernel, n, 512),
+            out_shape=[shape(2, rows, ff), shape(2, rows, ff), shape(2, deep, d), shape(8, 128, dtype=F32)],
+            in_specs=[any_] * 9,
+            out_specs=[vmem] * 4,
+            scratch_shapes=[
+                pltpu.VMEM((2, tokens, d), BF),
+                pltpu.VMEM((tokens, d), BF),
+                pltpu.VMEM((tokens, d), BF),
+                pltpu.VMEM((d, tokens), BF),
+                pltpu.VMEM((d, tokens), BF),
+                pltpu.VMEM((tokens, block), BF),
+                pltpu.VMEM((tokens, block), BF),
+                pltpu.VMEM((tokens, block), BF),
+                pltpu.VMEM((tokens, d), F32),
+                pltpu.VMEM((tokens, d), F32),
+                pltpu.VMEM((2, d, block), BF),
+                pltpu.VMEM((2, d, block), BF),
+                pltpu.VMEM((2, block, d), BF),
                 pltpu.VMEM((8, 128), F32),
                 pltpu.VMEM((n - 1, 8, 128), F32),
+                pltpu.SemaphoreType.DMA((3,)),
+                pltpu.SemaphoreType.DMA((2, 3)),
                 pltpu.SemaphoreType.DMA((n - 1,)),
                 pltpu.SemaphoreType.DMA((n - 1,)),
             ]
-            + Scatter.scratch(n, gu, wdb),
-            compiler_params=params(3),
-            name="backward0",
-        )(x, dh, *w0, gu1, wd1)
-
-        gradients = [
-            jnp.stack([gu0[:rows], gu1[:rows]]),
-            jnp.stack([gu0[rows:], gu1[rows:]]),
-            jnp.stack([wd0, wd1]),
-        ]
+            + Scatter.scratch(n, (2 * rows, block), (deep, d)),
+            compiler_params=params(2),
+            name="backward",
+        )(x, h, dy, *w0, *w1)
+
         count = n * sum(g.size for g in gradients)
         factor = jnp.minimum(1.0, 0.5 * lax.rsqrt(squares[0, 0] / count + 1e-30))
         new = [adamw(w.astype(F32), m, v, g.astype(F32) * factor) for w, m, v, g in zip(weights, m, v, gradients, strict=True)]

time: 325 us -> 288 us (0.89)
  Pallas kernels: 315 us -> 279 us
    pallas_call x2 -> x1, Pallas kernels: 210 us -> 175 us  [step(): pl.pallas_call(functools.partial(backward_kernel, n, 512), out_shape=[sha...]
where the time goes in v2:
time: 288 us
  Pallas kernels  279 us (97%)
  other arithmetic  5.9 us (2%)
    pallas_call x1, Pallas kernels, step(): pl.pallas_call(functools.partial(backward_kernel, n, 512), out_shape=[sha...  175 us
    pallas_call x1, Pallas kernels, step(): pl.pallas_call(functools.partial(gather_kernel, n, 0), out_shape=fulls, i...  52.9 us
    pallas_call x1, Pallas kernels, step(): pl.pallas_call(functools.partial(forward_kernel, n, 1, 256), out_shape=[s...  51.9 us
    convert_element_type x2, other arithmetic, adamw(): return ((w - 0.02 * step).astype(BF), m, v)  5.9 us

profile of v2, /device:TPU:21, one launch (start us, length us, event | category | flops | bytes accessed | tf_op | source)
XLA Modules:
  0.0 288.2 jit_solution(3558816562426160774)
XLA Ops:
  0.6 52.9 %gather0.1 = (bf16[16,40,2048]{2,1,0:T(8,128)(2,1)}, bf16[16,40,2048]{2,1,0:T(8,128)(2,1)}, bf16[16,128,640]{2,1,0:T(8,128)(2,1)}) custom-call(bf16[2,40,2048]{2,1,0:T(8,128)(2,1)} %sg.1, bf16[2,40,2048]{2,1,0:T(8,128)(2,1)} %su.1, bf16[2,128,640]{2,1,0:T(8,128)(2,1)} %sd.1), custom_call_target="tpu_custom_call" | custom-call | tf_op jit(solution)/shard_map/gather0/pallas_call | solution.py:513
  53.5 51.9 %forward0.1 = (bf16[2048,640]{1,0:T(8,128)(2,1)}, bf16[16,40,2048]{2,1,0:T(8,128)(2,1)}, bf16[16,40,2048]{2,1,0:T(8,128)(2,1)}, bf16[16,128,640]{2,1,0:T(8,128)(2,1)}) custom-call(bf16[2048,640]{1,0:T(8,128)(2,1)} %bitcast.9, bf16[640,2048]{1,0:T(8,128)(2,1)} %bitcast.11, bf16[640,2048]{1,0:T(8,128)(2,1)} %bitcast.13, bf16[2048,640]{1,0:T(8,128)(2,1)} %bitcast.15, ...), custom_call_target="tpu_custom_call" | custom-call | tf_op jit(solution)/shard_map/forward0/pallas_call | solution.py:523
  105.4 174.8 %backward.1 = (bf16[2,40,2048]{2,1,0:T(8,128)(2,1)}, bf16[2,40,2048]{2,1,0:T(8,128)(2,1)}, bf16[2,128,640]{2,1,0:T(8,128)(2,1)}, f32[8,128]{1,0:T(8,128)}) custom-call(bf16[2048,640]{1,0:T(8,128)(2,1)} %bitcast.10, bf16[2048,640]{1,0:T(8,128)(2,1)} %get-tuple-element.23.h, bf16[2048,640]{1,0:T(8,128)(2,1)} %bitcast.17, bf16[640,2048]{1,0:T(8,128)(2,1)} %bitcast.12, ...), custom_call_target="tpu_custom_call" | custom-call | tf_op jit(solution)/shard_map/backward/pallas_call | solution.py:535
  280.1 0.0 copy-start
  280.2 0.0 copy-start.1
  280.2 0.0 copy-start.2
  280.2 0.0 copy-start.3
  280.2 0.0 copy-start.4
  280.2 0.0 copy-start.5
  280.2 0.0 copy-start.6
  280.2 1.3 slice.3
  282.3 2.8 fusion.8
  285.1 0.0 copy-done
  285.1 0.0 copy-done.1
  285.1 0.0 copy-done.2
  285.1 0.0 copy-done.3
  285.1 0.0 copy-done.4
  285.1 0.0 copy-done.5
  285.1 0.0 copy-done.6
  285.1 3.1 %fusion.2 = (bf16[2,40,2048]{2,1,0:T(8,128)(2,1)}, f32[2,40,2048]{2,1,0:T(8,128)}, f32[2,40,2048]{2,1,0:T(8,128)}, bf16[2,40,2048]{2,1,0:T(8,128)(2,1)}, f32[2,40,2048]{2,1,0:T(8,128)}, /*index=5*/f32[2,40,2048]{2,1,0:T(8,128)}) fusion(bf16[2,40,2048]{2,1,0:T(8,128)(2,1)S(1)} %copy-done, f32[]{:T(128)} %bitcast.8, bf16[2,40,2048]{2,1,0:T(8,128)(2,1)S(1)} %copy-done.6, ...), kind=kLoop, calls=%fused_computation.11 | loop fusion | flops 5570560 | bytes 7208964 | tf_op jit(solution)/shard_map/convert_element_type | solution.py:491
Async XLA Ops:
  280.1 4.9 %copy-start = (bf16[2,40,2048]{2,1,0:T(8,128)(2,1)S(1)}, bf16[2,40,2048]{2,1,0:T(8,128)(2,1)}, u32[]{:S(2)}) copy-start(bf16[2,40,2048]{2,1,0:T(8,128)(2,1)} %sg.1) | copy-start | bytes 983044
  280.2 4.9 %copy-start.1 = (bf16[2,40,2048]{2,1,0:T(8,128)(2,1)S(1)}, bf16[2,40,2048]{2,1,0:T(8,128)(2,1)}, u32[]{:S(2)}) copy-start(bf16[2,40,2048]{2,1,0:T(8,128)(2,1)} %su.1) | copy-start | bytes 983044
  280.2 4.9 %copy-start.2 = (f32[2,40,2048]{2,1,0:T(8,128)S(1)}, f32[2,40,2048]{2,1,0:T(8,128)}, u32[]{:S(2)}) copy-start(f32[2,40,2048]{2,1,0:T(8,128)} %param.19) | copy-start | bytes 1966084
  280.2 4.9 %copy-start.3 = (f32[2,40,2048]{2,1,0:T(8,128)S(1)}, f32[2,40,2048]{2,1,0:T(8,128)}, u32[]{:S(2)}) copy-start(f32[2,40,2048]{2,1,0:T(8,128)} %param.16) | copy-start | bytes 1966084
  280.2 4.9 %copy-start.4 = (f32[2,40,2048]{2,1,0:T(8,128)S(1)}, f32[2,40,2048]{2,1,0:T(8,128)}, u32[]{:S(2)}) copy-start(f32[2,40,2048]{2,1,0:T(8,128)} %param.20) | copy-start | bytes 1966084
  280.2 4.9 %copy-start.5 = (f32[2,40,2048]{2,1,0:T(8,128)S(1)}, f32[2,40,2048]{2,1,0:T(8,128)}, u32[]{:S(2)}) copy-start(f32[2,40,2048]{2,1,0:T(8,128)} %param.17) | copy-start | bytes 1966084
  280.2 4.9 %copy-start.6 = (bf16[2,40,2048]{2,1,0:T(8,128)(2,1)S(1)}, bf16[2,40,2048]{2,1,0:T(8,128)(2,1)}, u32[]{:S(2)}) copy-start(bf16[2,40,2048]{2,1,0:T(8,128)(2,1)} %get-tuple-element.27) | copy-start | bytes 983044

commit v3 on v2

--- a/solution.py
+++ b/solution.py
@@ -76,37 +76,44 @@
             return ref.at[:, h * (cols // 2) : (h + 1) * (cols // 2)]
         return ref.at[h * (rows // 2) : (h + 1) * (rows // 2), :]
 
+    def slot(self, i, device):
+        rows = self.fulls[i].shape[0] // self.p.n
+        return self.fulls[i].at[pl.ds(pl.multiple_of(device * rows, rows), rows), :]
+
     def hop(self, i, way, t):
-        p, full = self.p, self.fulls[i]
+        p = self.p
         behind = (1 - t) if way == 0 else (t - 1)
-        ref = full.at[p.device(behind)]
+        ref = self.slot(i, p.device(behind))
         if t == self.half_hops:
             ref = self.half(ref, way)
         return remote(ref, ref, self.rs.at[i, way, t - 1], self.rr.at[i, way, t - 1], p.device(1 if way == 0 else -1))
 
     def landed(self, i, way, t):
-        p, full = self.p, self.fulls[i]
-        ref = full.at[p.device(-t if way == 0 else t)]
+        p = self.p
+        ref = self.slot(i, p.device(-t if way == 0 else t))
         if t == self.half_hops:
             ref = self.half(ref, way)
         return remote(ref, ref, self.rs.at[i, way, t - 1], self.rr.at[i, way, t - 1], p.device(1))
 
     def hand(self, i, k):
-        p, full = self.p, self.fulls[i]
+        p = self.p
         offset = 0 if k == 0 else (-(k + 1) // 2 if k % 2 else k // 2)
-        ref = full.at[p.device(offset)]
+        ref = self.slot(i, p.device(offset))
         return remote(ref, ref, self.ps.at[i, k], self.pr.at[i, k], p.partner)
 
     def handed(self, i, k):
-        p, full = self.p, self.fulls[i]
+        p = self.p
         offset = 0 if k == 0 else (-(k + 1) // 2 if k % 2 else k // 2)
-        ref = full.at[p.at(offset) * 2 + (1 - p.core)]
+        ref = self.slot(i, p.at(offset) * 2 + (1 - p.core))
         return remote(ref, ref, self.ps.at[i, k], self.pr.at[i, k], p.partner)
 
-    def begin(self):
-        own = [pltpu.make_async_copy(s, f.at[self.p.me], self.local.at[i]) for i, (s, f) in enumerate(zip(self.shards, self.fulls))]
+    def load(self):
+        own = [pltpu.make_async_copy(s, self.slot(i, self.p.me), self.local.at[i]) for i, s in enumerate(self.shards)]
         for c in own:
             c.start()
+        return own
+
+    def begin(self, own):
         for i, c in enumerate(own):
             c.wait()
             self.hop(i, 0, 1).start()
@@ -126,10 +133,12 @@
         if t == last:
             self.hand(i, 2 * last - 1).start()
 
-    def finish(self):
+    def arrive(self):
         for i in range(len(self.fulls)):
             for k in range(self.p.chips):
                 self.handed(i, k).wait_recv()
+
+    def drain(self):
         for i in range(len(self.fulls)):
             for k in range(self.p.chips):
                 self.hand(i, k).wait_send()
@@ -138,24 +147,22 @@
                     self.hop(i, way, t).wait_send()
 
 
-def gather_kernel(n, layer, wg, wu, wd, fg, fu, fd, *sems):
+def forward_kernel(n, tile, x, sg, su, sd, y, fg, fu, fd, gg, gu, gd, *sems):
     p = Place(n)
+    per = len(sems) // 2
+    first = Gather(p, [w.at[0] for w in (sg, su, sd)], [fg, fu, fd], sems[:per])
+    second = Gather(p, [w.at[1] for w in (sg, su, sd)], [gg, gu, gd], sems[per:])
+    own = first.load(), second.load()
     greet([p.device(1), p.device(-1), p.partner])
-    g = Gather(p, [w.at[layer] for w in (wg, wu, wd)], [fg, fu, fd], sems)
-    g.begin()
-    for t, i in g.events():
-        g.forward(t, i)
-    g.finish()
-
-
-def forward_kernel(n, layer, tile, x, wg, wu, wd, sg, su, sd, y, fg, fu, fd, *sems):
-    p = Place(n)
-    greet([p.device(1), p.device(-1), p.partner])
-    g = Gather(p, [w.at[layer] for w in (sg, su, sd)], [fg, fu, fd], sems)
-    g.begin()
-    events = g.events()
+    first.begin(own[0])
+    events = first.events()
+    for t, i in events:
+        if (t, i) == (first.half_hops, 0):
+            second.begin(own[1])
+        first.forward(t, i)
+    first.arrive()
     tiles = x.shape[0] // tile
-    ff = wg.shape[1]
+    ff = fg.shape[1]
     width = 512
 
     def body(i, _):
@@ -164,22 +171,24 @@
         a = normed(h.astype(F32))
         out = None
         for c in range(0, ff, width):
-            gate = dot(a, wg[:, c : c + width])
-            up = dot(a, wu[:, c : c + width])
+            gate = dot(a, fg[:, c : c + width])
+            up = dot(a, fu[:, c : c + width])
             hid = (gate * jax.nn.sigmoid(gate) * up).astype(BF)
-            term = dot(hid, wd[c : c + width, :])
+            term = dot(hid, fd[c : c + width, :])
             out = term if out is None else out + term
         y[rows, :] = h + out.astype(BF)
         for k, (t, j) in enumerate(events):
             @pl.when(i == k)
             def _(t=t, j=j):
-                g.forward(t, j)
+                second.forward(t, j)
         return 0
 
     lax.fori_loop(0, tiles, body, 0)
     for t, j in events[tiles:]:
-        g.forward(t, j)
-    g.finish()
+        second.forward(t, j)
+    second.arrive()
+    first.drain()
+    second.drain()
 
 
 class Scatter:
@@ -208,10 +217,12 @@
             pltpu.SemaphoreType.DMA((chips, 2)),
         ]
 
-    def owner(self, b):
-        half = self.p.chips // 2
-        b = lax.rem(b, self.p.chips)
-        return lax.div(b, 2) + half * lax.rem(b, 2)
+    def owner(self, b, core):
+        return lax.rem(3 * b + core, self.p.chips)
+
+    def columns(self, b):
+        run = self.g_wd.shape[-2]
+        return [pl.ds(pl.multiple_of((2 * self.owner(b, c) + c) * run, run), run) for c in range(2)]
 
     def pair(self, b):
         p = self.p
@@ -262,7 +273,7 @@
                 self.s_gu[b, way, s, :, cols] = term.astype(BF)
             self.gu_copy(b, way, s).start()
 
-        owner = self.owner(b)
+        owner = self.owner(b, p.core)
         for way in range(2):
             far = 4 - s
 
@@ -284,16 +295,17 @@
         p = self.p
         b = lax.rem(chain, p.chips)
         layer = out_wd.shape[0] - 1 - lax.div(chain, p.chips)
-        owner = self.owner(b)
+        owner = self.owner(b, p.core)
         full = slice(None)
         width = self.g_gu.shape[-1]
         rows = self.g_gu.shape[-2] // 2
         for way in range(2):
             self.gu_copy(b, way, 3).wait_recv()
         total = self.own_gu(b, p.chip, full) + self.r_gu[b, 0, 3].astype(F32) + self.r_gu[b, 1, 3].astype(F32)
-        cols = pl.ds(pl.multiple_of(owner * width, width), width)
-        out_gate[layer, :, cols] = total[:rows].astype(BF)
-        out_up[layer, :, cols] = total[rows:].astype(BF)
+        for c, cols in enumerate(self.columns(b)):
+            run = slice(c * width // 2, (c + 1) * width // 2)
+            out_gate[layer, :, cols] = total[:rows, run].astype(BF)
+            out_up[layer, :, cols] = total[rows:, run].astype(BF)
 
         @pl.when(owner == p.chip)
         def _():
@@ -306,7 +318,7 @@
         b = lax.rem(chain, p.chips)
         for c in self.pair(b):
             c.wait_send()
-        owner = self.owner(b)
+        owner = self.owner(b, p.core)
         for way in range(2):
             for s in range(4):
                 self.gu_copy(b, way, s).wait_send()
@@ -337,14 +349,17 @@
     ]
 
     def fetch(b, weights):
-        cols = pl.ds(pl.multiple_of(sc.owner(b) * block, block), block)
         slot = lax.rem(b, 2)
         g, u, w = weights
-        return [
-            pltpu.make_async_copy(g.at[:, cols], bg.at[slot], w_sem.at[slot, 0]),
-            pltpu.make_async_copy(u.at[:, cols], bu.at[slot], w_sem.at[slot, 1]),
-            pltpu.make_async_copy(w.at[cols, :], bd.at[slot], w_sem.at[slot, 2]),
-        ]
+        copies = []
+        for c, cols in enumerate(sc.columns(b)):
+            run = slice(c * block // 2, (c + 1) * block // 2)
+            copies += [
+                pltpu.make_async_copy(g.at[:, cols], bg.at[slot, :, run], w_sem.at[slot, c, 0]),
+                pltpu.make_async_copy(u.at[:, cols], bu.at[slot, :, run], w_sem.at[slot, c, 1]),
+                pltpu.make_async_copy(w.at[cols, :], bd.at[slot, run, :], w_sem.at[slot, c, 2]),
+            ]
+        return copies
 
     first, second = (wg1, wu1, wd1), (wg0, wu0, wd0)
     for c in loads + fetch(0, first):
@@ -508,28 +523,17 @@
         tokens, d = x.shape
         rows, ff = wg.shape[1:]
         deep = wd.shape[1]
-        fulls = [shape(n, rows, ff), shape(n, rows, ff), shape(n, deep, d)]
-        flat = lambda f: (f[0].reshape(d, ff), f[1].reshape(d, ff), f[2].reshape(ff, d))
-        first = pl.pallas_call(
-            functools.partial(gather_kernel, n, 0),
-            out_shape=fulls,
-            in_specs=[any_] * 3,
-            out_specs=[vmem] * 3,
-            scratch_shapes=Gather.sems(n, 3),
-            compiler_params=params(0),
-            name="gather0",
-        )(wg, wu, wd)
-        w0 = flat(first)
-        h, *second = pl.pallas_call(
-            functools.partial(forward_kernel, n, 1, 256),
-            out_shape=[shape(tokens, d)] + fulls,
-            in_specs=[vmem] * 4 + [any_] * 3,
-            out_specs=[vmem] * 4,
-            scratch_shapes=Gather.sems(n, 3),
+        fulls = [shape(d, ff), shape(d, ff), shape(ff, d)]
+        h, *full = pl.pallas_call(
+            functools.partial(forward_kernel, n, 256),
+            out_shape=[shape(tokens, d)] + fulls + fulls,
+            in_specs=[vmem] + [any_] * 3,
+            out_specs=[vmem] * 7,
+            scratch_shapes=Gather.sems(n, 3) * 2,
             compiler_params=params(1),
-            name="forward0",
-        )(x, *w0, wg, wu, wd)
-        w1 = flat(second)
+            name="forward",
+        )(x, wg, wu, wd)
+        w0, w1 = full[:3], full[3:]
 
         block = ff // (n // 2)
         *gradients, squares = pl.pallas_call(
@@ -554,7 +558,7 @@
                 pltpu.VMEM((8, 128), F32),
                 pltpu.VMEM((n - 1, 8, 128), F32),
                 pltpu.SemaphoreType.DMA((3,)),
-                pltpu.SemaphoreType.DMA((2, 3)),
+                pltpu.SemaphoreType.DMA((2, 2, 3)),
                 pltpu.SemaphoreType.DMA((n - 1,)),
                 pltpu.SemaphoreType.DMA((n - 1,)),
             ]

time: 288 us -> 271 us (0.941)
  Pallas kernels: 279 us -> 262 us
    pallas_call x2 -> x1, Pallas kernels: 105 us -> 95 us  [step(): pl.pallas_call(functools.partial(forward_kernel, n, 256), out_shape=[shap...]
    pallas_call x1, Pallas kernels: 175 us -> 167 us  [step(): pl.pallas_call(functools.partial(backward_kernel, n, 512), out_shape=[sha...]
where the time goes in v3:
time: 271 us
  Pallas kernels  262 us (97%)
  other arithmetic  5.9 us (2%)
    pallas_call x1, Pallas kernels, step(): pl.pallas_call(functools.partial(backward_kernel, n, 512), out_shape=[sha...  167 us
    pallas_call x1, Pallas kernels, step(): pl.pallas_call(functools.partial(forward_kernel, n, 256), out_shape=[shap...  95 us
    convert_element_type x2, other arithmetic, adamw(): return ((w - 0.02 * step).astype(BF), m, v)  5.9 us

profile of v3, /device:TPU:21, one launch (start us, length us, event | category | flops | bytes accessed | tf_op | source)
XLA Modules:
  0.0 271.0 jit_solution(7197730990212613208)
XLA Ops:
  0.6 95.0 %forward.1 = (bf16[2048,640]{1,0:T(8,128)(2,1)}, bf16[640,2048]{1,0:T(8,128)(2,1)}, bf16[640,2048]{1,0:T(8,128)(2,1)}, bf16[2048,640]{1,0:T(8,128)(2,1)}, bf16[6...) custom-call(bf16[2048,640]{1,0:T(8,128)(2,1)} %bitcast.3, bf16[2,40,2048]{2,1,0:T(8,128)(2,1)} %sg.1, ...), custom_call_target="tpu_custom_call" | custom-call | tf_op jit(solution)/shard_map/forward/pallas_call | solution.py:527
  95.7 167.3 %backward.1 = (bf16[2,40,2048]{2,1,0:T(8,128)(2,1)}, bf16[2,40,2048]{2,1,0:T(8,128)(2,1)}, bf16[2,128,640]{2,1,0:T(8,128)(2,1)}, f32[8,128]{1,0:T(8,128)}) custom-call(bf16[2048,640]{1,0:T(8,128)(2,1)} %bitcast.4, bf16[2048,640]{1,0:T(8,128)(2,1)} %get-tuple-element.20.h, bf16[2048,640]{1,0:T(8,128)(2,1)} %bitcast.5, ...), custom_call_target="tpu_custom_call" | custom-call | tf_op jit(solution)/shard_map/backward/pallas_call | solution.py:539
  263.0 0.0 copy-start
  263.0 0.0 copy-start.1
  263.0 0.0 copy-start.2
  263.0 0.0 copy-start.3
  263.0 0.0 copy-start.4
  263.0 0.0 copy-start.5
  263.0 0.0 copy-start.6
  263.1 1.3 slice.3
  265.1 2.8 %fusion.8 = (bf16[2,128,640]{2,1,0:T(8,128)(2,1)}, f32[2,128,640]{2,1,0:T(8,128)}, f32[2,128,640]{2,1,0:T(8,128)}) fusion(bf16[2,128,640]{2,1,0:T(8,128)(2,1)} %sd.1, f32[]{:T(128)} %bitcast.2, bf16[2,128,640]{2,1,0:T(8,128)(2,1)} %get-tuple-element.30, f32[2,128,640]{2,1,0:T(8,128)} %param.21, f32[2,128,640]{2,1,0:T(8,128)} %param.18), kind=kLoop, calls=%fused_computation.17 | loop fusion | flops 2785280 | bytes 3604484 | tf_op jit(solution)/shard_map/convert_element_type | solution.py:506
  267.9 0.0 copy-done
  267.9 0.0 copy-done.1
  267.9 0.0 copy-done.2
  267.9 0.0 copy-done.3
  267.9 0.0 copy-done.4
  267.9 0.0 copy-done.5
  267.9 0.0 copy-done.6
  268.0 3.1 %fusion.2 = (bf16[2,40,2048]{2,1,0:T(8,128)(2,1)}, f32[2,40,2048]{2,1,0:T(8,128)}, f32[2,40,2048]{2,1,0:T(8,128)}, bf16[2,40,2048]{2,1,0:T(8,128)(2,1)}, f32[2,40,2048]{2,1,0:T(8,128)}, /*index=5*/f32[2,40,2048]{2,1,0:T(8,128)}) fusion(bf16[2,40,2048]{2,1,0:T(8,128)(2,1)S(1)} %copy-done, f32[]{:T(128)} %bitcast.2, bf16[2,40,2048]{2,1,0:T(8,128)(2,1)S(1)} %copy-done.6, ...), kind=kLoop, calls=%fused_computation.11 | loop fusion | flops 5570560 | bytes 7208964 | tf_op jit(solution)/shard_map/convert_element_type | solution.py:506
Async XLA Ops:
  263.0 4.9 %copy-start = (bf16[2,40,2048]{2,1,0:T(8,128)(2,1)S(1)}, bf16[2,40,2048]{2,1,0:T(8,128)(2,1)}, u32[]{:S(2)}) copy-start(bf16[2,40,2048]{2,1,0:T(8,128)(2,1)} %sg.1) | copy-start | bytes 983044
  263.0 4.9 %copy-start.1 = (bf16[2,40,2048]{2,1,0:T(8,128)(2,1)S(1)}, bf16[2,40,2048]{2,1,0:T(8,128)(2,1)}, u32[]{:S(2)}) copy-start(bf16[2,40,2048]{2,1,0:T(8,128)(2,1)} %su.1) | copy-start | bytes 983044
  263.0 4.9 %copy-start.2 = (f32[2,40,2048]{2,1,0:T(8,128)S(1)}, f32[2,40,2048]{2,1,0:T(8,128)}, u32[]{:S(2)}) copy-start(f32[2,40,2048]{2,1,0:T(8,128)} %param.19) | copy-start | bytes 1966084
  263.0 4.9 %copy-start.3 = (f32[2,40,2048]{2,1,0:T(8,128)S(1)}, f32[2,40,2048]{2,1,0:T(8,128)}, u32[]{:S(2)}) copy-start(f32[2,40,2048]{2,1,0:T(8,128)} %param.16) | copy-start | bytes 1966084
  263.0 4.9 %copy-start.4 = (f32[2,40,2048]{2,1,0:T(8,128)S(1)}, f32[2,40,2048]{2,1,0:T(8,128)}, u32[]{:S(2)}) copy-start(f32[2,40,2048]{2,1,0:T(8,128)} %param.20) | copy-start | bytes 1966084
  263.0 4.9 %copy-start.5 = (f32[2,40,2048]{2,1,0:T(8,128)S(1)}, f32[2,40,2048]{2,1,0:T(8,128)}, u32[]{:S(2)}) copy-start(f32[2,40,2048]{2,1,0:T(8,128)} %param.17) | copy-start | bytes 1966084
  263.0 4.9 %copy-start.6 = (bf16[2,40,2048]{2,1,0:T(8,128)(2,1)S(1)}, bf16[2,40,2048]{2,1,0:T(8,128)(2,1)}, u32[]{:S(2)}) copy-start(bf16[2,40,2048]{2,1,0:T(8,128)(2,1)} %get-tuple-element.27) | copy-start | bytes 983044
